TPU v7x, 256 devices: a whole 4x4x8 slice. The times are simulated.
256 devices in a mesh: tm: 32 (over y, z), space: 8 (over x, core).
Axes of the slice: x: 4, y: 4, z: 8, core: 2. Of those that a mesh axis runs over, the one named last changes fastest.
Arguments:
- forcing: float32 [128, 128, 128, 128], P('tm', 'space'), may hold values from -6 to 6
- coarse_guess: float32 [32, 128, 128, 128], P('tm', 'space'), may hold values from -6 to 6
- initial: float32 [128, 128, 128], P('space'), may hold values from -6 to 6
Outputs:
- solution: float32 [128, 128, 128, 128], P('tm', 'space')
- residual: float32 [32, 128, 128, 128], P('tm', None, 'space')
All inputs are finite; a program needn't handle non-finite values.
Results may differ from a plain program's by a relative error of at most 0.00007.
Values sent between devices are 32-bit elements; how exact they have to be, the bound alone decides.
A program may use at most 192 MiB of HBM per device.

v0:
```python
import jax
import jax.numpy as jnp
from jax import lax
from jax.sharding import Mesh
from jax.sharding import PartitionSpec as P

TM = ("tm_0", "tm_1")


time_step = 0.5
highest = lax.Precision.HIGHEST


def grouped_exchange(shard, axis, split_dim, concat_dim, work, item_dim, out_dim):

    def moved(group):
        return lax.all_to_all(group, axis, split_axis=split_dim, concat_axis=concat_dim, tiled=True)

    items = jax.tree.leaves(shard)[0].shape[item_dim]
    ends = [items * k // 2 for k in range(2 + 1)] if items % 2 == 0 else [0, items]
    groups = [
        jax.tree.map(lambda a: lax.slice_in_dim(a, low, high, axis=item_dim), shard)
        for low, high in zip(ends, ends[1:])
    ]
    arrived = [moved(group) for group in groups]
    made = [work(group) for group in arrived]
    return jax.tree.map(lambda *parts: jnp.concatenate(parts, axis=out_dim), *made)


def from_behind(shard, axis, by):
    devices = lax.axis_size(axis)
    return lax.ppermute(shard, axis, [(i, (i + by) % devices) for i in range(devices)])


def passed_along(value, axis, steps):
    count = lax.axis_size(axis)
    first, last = (max(0, -steps), min(count, count - steps))
    return lax.ppermute(value, axis, [(source, source + steps) for source in range(first, last)])


def filled_with(shard, identity):
    return jax.tree.map(
        lambda part, zero: jnp.zeros_like(part) + jnp.asarray(zero, part.dtype), shard, identity
    )


def prefix_by_axis(shard, axes, combine, identity):
    before = start = filled_with(shard, identity)
    running = shard
    for axis in reversed(axes):
        devices, here = (lax.axis_size(axis), lax.axis_index(axis))
        pieces = jax.tree.map(lambda part: lax.all_gather(part, axis), running)
        inside, running = (start, start)
        for k in range(devices):
            passed = k < here
            running = combine(running, jax.tree.map(lambda part: part[k], pieces))
            inside = jax.tree.map(lambda new, old: jnp.where(passed, new, old), running, inside)
        before = combine(inside, before)
    return before


def sine_table(length):
    ladder = jnp.arange(1, length + 1, dtype=jnp.float32)
    return jnp.sqrt(2.0 / (length + 1)) * jnp.sin(
        jnp.pi * ladder[:, None] * ladder[None, :] / (length + 1)
    )


def eigen_values(length):
    ladder = jnp.arange(1, length + 1, dtype=jnp.float32)
    return -4.0 * jnp.sin(jnp.pi * ladder / (2 * (length + 1))) ** 2


def per_device(forcing, coarse_guess, initial):
    steps = forcing.shape[0]
    width_x = initial.shape[0] * lax.axis_size("space")
    width_y = initial.shape[1]
    width_z = initial.shape[2]
    slice_y = width_y // lax.axis_size("space")
    table_x = sine_table(width_x)
    table_y = sine_table(width_y)
    table_z = sine_table(width_z)
    offset = lax.axis_index("space") * slice_y
    local_y = lax.dynamic_slice_in_dim(eigen_values(width_y), offset, slice_y)
    spectrum = (
        eigen_values(width_x)[:, None, None]
        + local_y[None, :, None]
        + eigen_values(width_z)[None, None, :]
    )
    implicit = 1.0 - 0.5 * time_step * spectrum
    fine_rate = (1.0 + 0.5 * time_step * spectrum) / implicit
    wide_step = 0.5 * steps * time_step
    coarse_rate = (1.0 + wide_step * spectrum) / (1.0 - wide_step * spectrum)
    leading = (lax.axis_index(TM) == 0).astype(jnp.float32)
    fields = jnp.concatenate([forcing, coarse_guess, initial[None]], axis=0)
    fields = jnp.einsum("bxyz,zr->bxyr", fields, table_z, precision=highest)
    fields = jnp.einsum("bxyr,yq->bxqr", fields, table_y, precision=highest)

    def along_first(pieces):
        return jnp.einsum("bxqr,xp->bpqr", pieces, table_x, precision=highest)

    spectra = grouped_exchange(fields, "space", 2, 1, along_first, 0, 0)
    anchor = leading * spectra[steps + 1]
    begin = from_behind(spectra[steps], TM, 1)
    source = spectra[:steps] * (time_step / implicit)

    def relax_steps(starting):
        current = starting
        values = []
        for number in range(steps - 1):
            current = fine_rate * current + source[number]
            values.append(current)
        return values

    coarse_value = fine_rate * relax_steps(begin)[-1] + source[steps - 1]
    second = passed_along(coarse_value, TM, 1) + anchor
    residual = fine_rate * relax_steps(second)[-1] + source[steps - 1] - coarse_value

    def combine(earlier, later):
        return (earlier[0] * later[0], later[0] * earlier[1] + later[1])

    identity = (jnp.ones_like(residual), jnp.zeros_like(residual))
    powers, prefix = prefix_by_axis((coarse_rate, residual), TM, combine, identity)
    corrected = coarse_value + (coarse_rate * prefix + residual)
    third = second + prefix
    points = relax_steps(third) + [corrected]
    fields = jnp.stack(points, axis=0)
    fields = jnp.einsum("bpqr,px->bxqr", fields, table_x, precision=highest)
    pieces = lax.all_to_all(fields, "space", split_axis=1, concat_axis=2, tiled=True)
    pieces = jnp.einsum("bxqr,qy->bxyr", pieces, table_y, precision=highest)
    return (jnp.einsum("bxyr,rz->bxyz", pieces, table_z, precision=highest), residual[None])


def solution(mesh):
    torus = Mesh(mesh.devices.reshape(4, 8, mesh.shape["space"]), ("tm_0", "tm_1", "space"))
    in_specs = (P(TM, "space", None, None), P(TM, "space", None, None), P("space", None, None))
    out_specs = (P(TM, "space", None, None), P(TM, None, "space", None))
    return jax.shard_map(
        per_device, mesh=torus, in_specs=in_specs, out_specs=out_specs, check_vma=False
    )
```

profile of v0, /device:TPU:1, one launch (start us, length us, event | category | flops | bytes accessed | tf_op | source)
XLA Modules:
  0.0 471.3 jit_solution(15251944645093215695)
XLA Ops:
  7.2 0.0 all-gather.6.cloned.1.call-start
  7.3 0.1 dynamic_slice.3
  7.3 0.1 broadcast_add_fusion
  7.4 0.1 copy.57
  7.5 1.4 fusion.24
  8.9 0.0 all-gather.6.cloned.1.call-update
  8.9 8.0 %fusion = f32[6,16,128,128]{3,2,1,0:T(8,128)S(1)} fusion(f32[1,16,128,128]{3,2,1,0:T(8,128)} %bitcast.260, f32[1,16,128,128]{3,2,1,0:T(8,128)} %param.4, f32[4,16,128,128]{3,2,1,0:T(8,128)} %param.3, f32[128]{0:T(128)S(1)} %get-tuple-element.35, f32[128]{0:T(128)S(1)} %get-tuple-element.36), kind=kOutput, calls=%fused_computation | convolution fusion | flops 2419113984 | bytes 12583936 | tf_op jit(solution)/shard_map/bxyz,zr->bxyr/dot_general | solution.py:96
  16.9 6.5 %convolution_bitcast_fusion = f32[6,16,128,128]{3,2,1,0:T(8,128)S(1)} fusion(f32[6,16,128,128]{3,2,1,0:T(8,128)S(1)} %fusion, f32[128]{0:T(128)S(1)} %get-tuple-element.35, f32[128]{0:T(128)S(1)} %get-tuple-element.36), kind=kOutput, calls=%fused_computation.18 | convolution fusion | flops 2415968256 | bytes 12583936 | tf_op jit(solution)/shard_map/bxyr,yq->bxqr/dot_general | solution.py:97
  23.4 2.1 fusion.114
  25.5 3.5 copy.51
  29.0 7.1 %all-to-all-start = ((f32[3,16,128,128]{3,1,0,2:T(8,128)}), f32[3,16,128,128]{3,1,0,2:T(8,128)S(1)}, u32[]{:S(2)}, u32[]{:S(2)}) async-start(f32[3,16,128,128]{3,1,0,2:T(8,128)} %copy.51), calls=%async_computation | async-start | bytes 6291456 | tf_op jit(solution)/shard_map/all_to_all | solution.py:17
  36.1 5.3 %copy.54 = f32[3,16,128,128]{3,1,0,2:T(8,128)} copy(f32[3,16,128,128]{3,2,1,0:T(8,128)} %get-tuple-element.23) | data formatting | bytes 6291456 | tf_op jit(solution)/shard_map/slice | solution.py:22
  41.5 32.1 %all-to-all-done = f32[3,16,128,128]{3,1,0,2:T(8,128)S(1)} async-done(((f32[3,16,128,128]{3,1,0,2:T(8,128)}), f32[3,16,128,128]{3,1,0,2:T(8,128)S(1)}, u32[]{:S(2)}, u32[]{:S(2)}) %all-to-all-start) | async-done | bytes 3145760 | tf_op jit(solution)/shard_map/all_to_all | solution.py:17
  73.6 5.3 %all-to-all-start.1 = ((f32[3,16,128,128]{3,1,0,2:T(8,128)}), f32[3,16,128,128]{3,1,0,2:T(8,128)}, u32[]{:S(2)}, u32[]{:S(2)}) async-start(f32[3,16,128,128]{3,1,0,2:T(8,128)} %copy.54), calls=%async_computation.1 | async-start | bytes 6291456 | tf_op jit(solution)/shard_map/all_to_all | solution.py:17
  78.9 0.0 all-gather.12.cloned.1.call-start
  78.9 0.4 copy.52
  79.4 3.2 convolution_bitcast_fusion.2
  82.5 1.1 slice_bitcast_fusion.4
  83.6 0.3 collective-permute-start
  83.9 1.3 fusion.22
  85.2 31.3 %all-to-all-done.1 = f32[3,16,128,128]{3,1,0,2:T(8,128)} async-done(((f32[3,16,128,128]{3,1,0,2:T(8,128)}), f32[3,16,128,128]{3,1,0,2:T(8,128)}, u32[]{:S(2)}, u32[]{:S(2)}) %all-to-all-start.1) | async-done | bytes 3145760 | tf_op jit(solution)/shard_map/all_to_all | solution.py:17
  116.5 2.3 copy.55
  118.8 0.0 copy-start.8
  118.8 3.3 convolution_bitcast_fusion.1
  122.1 0.0 copy-done.8
  122.1 0.7 fusion.6
  122.8 0.0 copy-start
  122.8 9.2 %collective-permute-done = f32[128,16,128]{2,0,1:T(8,128)} collective-permute-done((f32[128,16,128]{2,0,1:T(8,128)}, f32[128,16,128]{2,0,1:T(8,128)}, u32[]{:S(2)}, u32[]{:S(2)}) %collective-permute-start) | collective-permute-done | bytes 1048608 | tf_op jit(solution)/shard_map/ppermute | solution.py:32
  132.0 0.0 copy-done
  132.0 2.9 multiply_add_fusion.2
  134.9 2.2 collective-permute-start.1
  137.2 21.7 %collective-permute-done.1 = f32[128,16,128]{2,0,1:T(8,128)} collective-permute-done((f32[128,16,128]{2,0,1:T(8,128)}, f32[128,16,128]{2,0,1:T(8,128)}, u32[]{:S(2)}, u32[]{:S(2)}) %collective-permute-start.1) | collective-permute-done | bytes 1048608 | tf_op jit(solution)/shard_map/ppermute | solution.py:38
  158.8 4.6 add_subtract_fusion.2
  163.5 0.0 all-gather.12.cloned.1.call-update
  163.5 0.0 all-gather.8.cloned.1.call-start
  163.6 0.0 all-gather.6.cloned.1.call-done
  163.6 6.9 %fusion.113 = (f32[1,128,16,128]{3,2,1,0:T(8,128)}, f32[1,128,16,128]{3,2,1,0:T(8,128)}, f32[1,128,16,128]{3,2,1,0:T(8,128)}, f32[1,128,16,128]{3,2,1,0:T(8,128)...) fusion(f32[8,128,16,128]{3,2,1,0:T(8,128)} %all-gather.6.cloned, ...), kind=kLoop, calls=%fused_computation.168 | loop fusion | bytes 16777216 | tf_op jit(solution)/shard_map/slice | solution.py:56
  170.5 87.6 %all-gather.12.cloned.1.call-done = f32[1024,16,128]{2,0,1:T(8,128)} async-done(((f32[128,16,128]{2,0,1:T(8,128)}), f32[1024,16,128]{2,0,1:T(8,128)}) %all-gather.12.cloned.1.call-update) | async-done | bytes 8388624 | tf_op jit(solution)/shard_map/all_gather | solution.py:52
  258.1 8.4 %multiply_multiply_fusion = (f32[1,128,16,128]{3,1,2,0:T(8,128)S(1)}, f32[1,128,16,128]{3,1,2,0:T(8,128)}) fusion(f32[1,128,16,128]{3,2,1,0:T(8,128)} %get-tuple-element.22, f32[1,128,16,128]{3,2,1,0:T(8,128)} %get-tuple-element.16, f32[1,128,16,128]{3,2,1,0:T(8,128)} %get-tuple-element.17, f32[1,128,16,128]{3,2,1,0:T(8,128)} %get-tuple-element.18, ...), kind=kLoop, calls=%fused_computation.108 | loop fusion | flops 6029312 | bytes 18874368 | tf_op jit(solution)/shard_map/mul | solution.py:120
  266.4 1.6 copy.66
  268.0 0.0 all-gather.8.cloned.1.call-update
  268.1 0.0 all-gather.10.cloned.1.call-start
  268.1 2.8 copy.71
  270.9 0.0 all-gather.10.cloned.1.call-update
  271.0 46.6 %all-gather.8.cloned.1.call-done = f32[4,128,16,128]{3,2,1,0:T(8,128)} async-done(((f32[1,128,16,128]{3,2,1,0:T(8,128)}), f32[4,128,16,128]{3,2,1,0:T(8,128)}) %all-gather.8.cloned.1.call-update) | async-done | bytes 4194320 | tf_op jit(solution)/shard_map/all_gather | solution.py:52
  317.6 4.3 fusion.115
  321.9 48.5 %all-gather.10.cloned.1.call-done = f32[4,128,16,128]{3,2,1,0:T(8,128)} async-done(((f32[1,128,16,128]{3,2,1,0:T(8,128)}), f32[4,128,16,128]{3,2,1,0:T(8,128)}) %all-gather.10.cloned.1.call-update) | async-done | bytes 4194320 | tf_op jit(solution)/shard_map/all_gather | solution.py:52
  370.4 2.6 fusion.116
  373.1 0.8 copy-done.1
  373.9 0.3 copy-done.4
  374.2 0.3 copy-done.5
  374.5 0.3 copy-done.6
  374.8 0.3 copy-done.7
  375.1 12.0 %fusion.59 = (f32[1,128,16,128]{3,1,2,0:T(8,128)S(1)}, f32[128,16,128]{2,0,1:T(8,128)S(1)}, f32[128,16,128]{2,0,1:T(8,128)S(1)}) fusion(f32[4,128,16,128]{3,1,2,0:T(8,128)S(1)} %copy-done.1, f32[128]{0:T(128)S(1)} %multiply_multiply_fusion.1, f32[128,16]{0,1:T(8,128)S(1)} %broadcast_add_fusion, f32[128,16,128]{2,0,1:T(8,128)} %collective-permute-done.1, ...), kind=kLoop, calls=%fused_computation.110 | loop fusion | flops 17039360 | bytes 32514576 | tf_op jit(solution)/shard_map/stack | solution.py:127
  387.0 0.0 copy-done.2
  387.1 2.1 add_bitcast_fusion
  389.1 4.1 fusion.17
  393.2 4.4 copy.77
  397.7 5.7 %all-to-all-start.2 = ((f32[4,128,16,128]{3,2,0,1:T(8,128)}), f32[4,128,16,128]{3,2,0,1:T(8,128)}, u32[]{:S(2)}, u32[]{:S(2)}) async-start(f32[4,128,16,128]{3,2,0,1:T(8,128)} %copy.77), calls=%async_computation.2 | async-start | bytes 8388608 | tf_op jit(solution)/shard_map/all_to_all | solution.py:129
  403.4 1.6 copy.81
  405.0 47.2 %all-to-all-done.2 = f32[4,128,16,128]{3,2,0,1:T(8,128)} async-done(((f32[4,128,16,128]{3,2,0,1:T(8,128)}), f32[4,128,16,128]{3,2,0,1:T(8,128)}, u32[]{:S(2)}, u32[]{:S(2)}) %all-to-all-start.2) | async-done | bytes 4194336 | tf_op jit(solution)/shard_map/all_to_all | solution.py:129
  452.1 2.8 copy.79
  454.9 4.1 fusion.66
  459.0 5.5 %fusion.15 = f32[4,16,128,128]{3,2,1,0:T(8,128)} fusion(f32[128,4,16,128]{3,0,2,1:T(8,128)S(1)} %fusion.66, f32[128]{0:T(128)S(1)} %get-tuple-element.35, f32[128]{0:T(128)S(1)} %get-tuple-element.36), kind=kOutput, calls=%fused_computation.16 | convolution fusion | flops 1610661888 | bytes 8389632 | tf_op jit(solution)/shard_map/bxyr,rz->bxyz/dot_general | solution.py:131
  (10 shorter events, 0.1 us)
Async XLA Ops:
  7.2 156.4 %all-gather.6.cloned.1.call-start = ((), (), s32[]{:S(2)}) async-start(), calls=%async_computation.3 | async-start | bytes 9437184 | tf_op jit(solution)/shard_map/all_gather | solution.py:52
  29.0 44.6 %all-to-all-start = ((f32[3,16,128,128]{3,1,0,2:T(8,128)}), f32[3,16,128,128]{3,1,0,2:T(8,128)S(1)}, u32[]{:S(2)}, u32[]{:S(2)}) async-start(f32[3,16,128,128]{3,1,0,2:T(8,128)} %copy.51), calls=%async_computation | async-start | bytes 6291456 | tf_op jit(solution)/shard_map/all_to_all | solution.py:17
  73.6 42.9 %all-to-all-start.1 = ((f32[3,16,128,128]{3,1,0,2:T(8,128)}), f32[3,16,128,128]{3,1,0,2:T(8,128)}, u32[]{:S(2)}, u32[]{:S(2)}) async-start(f32[3,16,128,128]{3,1,0,2:T(8,128)} %copy.54), calls=%async_computation.1 | async-start | bytes 6291456 | tf_op jit(solution)/shard_map/all_to_all | solution.py:17
  78.9 179.2 %all-gather.12.cloned.1.call-start = ((), (), s32[]{:S(2)}) async-start(), calls=%async_computation.6 | async-start | bytes 9437184 | tf_op jit(solution)/shard_map/all_gather | solution.py:52
  83.6 48.4 %collective-permute-start = (f32[128,16,128]{2,0,1:T(8,128)}, f32[128,16,128]{2,0,1:T(8,128)}, u32[]{:S(2)}, u32[]{:S(2)}) collective-permute-start(f32[128,16,128]{2,0,1:T(8,128)} %slice_bitcast_fusion.4), channel_id=1, source_target_pairs={{0,8},{8,16},{16,24},{24,32},{32,40},{40,48},{48,56},{56,64},{64,7... | collective-permute-start | bytes 3145736 | tf_op jit(solution)/shard_map/ppermute | solution.py:32
  118.8 3.3 copy-start.8
  122.8 9.2 %copy-start = (f32[4,128,16,128]{3,1,2,0:T(8,128)}, f32[4,128,16,128]{3,1,2,0:T(8,128)S(1)}, u32[]{:S(2)}) copy-start(f32[4,128,16,128]{3,1,2,0:T(8,128)S(1)} %fusion.6) | copy-start | bytes 12582916
  134.9 23.9 %collective-permute-start.1 = (f32[128,16,128]{2,0,1:T(8,128)}, f32[128,16,128]{2,0,1:T(8,128)}, u32[]{:S(2)}, u32[]{:S(2)}) collective-permute-start(f32[128,16,128]{2,0,1:T(8,128)} %multiply_add_fusion.2), channel_id=1, source_target_pairs={{0,8},{8,16},{16,24},{24,32},{32,40},{40,48},{48,56},{56,64},{64,7... | collective-permute-start | bytes 3145736 | tf_op jit(solution)/shard_map/ppermute | solution.py:38
  163.5 154.1 %all-gather.8.cloned.1.call-start = ((), (), s32[]{:S(2)}) async-start(), calls=%async_computation.4 | async-start | bytes 5242880 | tf_op jit(solution)/shard_map/all_gather | solution.py:52
  268.1 102.4 %all-gather.10.cloned.1.call-start = ((), (), s32[]{:S(2)}) async-start(), calls=%async_computation.5 | async-start | bytes 5242880 | tf_op jit(solution)/shard_map/all_gather | solution.py:52
  370.4 3.4 copy-start.1
  370.4 3.7 copy-start.4
  370.4 4.1 copy-start.5
  370.4 4.4 copy-start.6
  370.4 4.7 copy-start.7
  375.1 12.0 %copy-start.2 = (f32[128,16,128]{2,0,1:T(8,128)S(1)}, f32[128,16,128]{2,0,1:T(8,128)}, u32[]{:S(2)}) copy-start(f32[128,16,128]{2,0,1:T(8,128)} %add_subtract_fusion.2) | copy-start | bytes 3145732
  397.7 5.7 %copy-start.3 = (f32[128,16,128]{2,0,1:T(8,128)S(1)}, f32[128,16,128]{2,0,1:T(8,128)}, u32[]{:S(2)}) copy-start(f32[128,16,128]{2,0,1:T(8,128)} %add_subtract_fusion.2) | copy-start | bytes 3145732
  397.7 54.4 %all-to-all-start.2 = ((f32[4,128,16,128]{3,2,0,1:T(8,128)}), f32[4,128,16,128]{3,2,0,1:T(8,128)}, u32[]{:S(2)}, u32[]{:S(2)}) async-start(f32[4,128,16,128]{3,2,0,1:T(8,128)} %copy.77), calls=%async_computation.2 | async-start | bytes 8388608 | tf_op jit(solution)/shard_map/all_to_all | solution.py:129
Sparse Core Ops, SparseCore 0:
  9.8 115.1 all-gather.5
  163.6 94.4 all-gather.11
  268.2 49.3 all-gather.7
  319.3 51.1 all-gather.9
where the time goes:
time: 481 us; the launch traced here: 471 us
  waiting for transfers between devices  324 us (67%)
  local copies, waits for them, and re-layouts  44 us (9%)
  matrix products  34.6 us (7%)
  other arithmetic  33.4 us (7%)
  starting transfers between devices  20.7 us (4%)
  between operations  14.2 us (3%)
    all_gather x4, waiting for transfers between devices, prefix_by_axis(): pieces = jax.tree.map(lambda part: lax.all_gather(part, axis), running)  183 us
    all_to_all x2, waiting for transfers between devices, moved(): lax.all_to_all(group, axis, split_axis=split_dim, concat_axis=concat_dim,...  63.4 us
    all_to_all x1, waiting for transfers between devices, per_device(): lax.all_to_all(fields, 'space', split_axis=1, concat_axis=2, tiled=True)  47.2 us
    ppermute x1, waiting for transfers between devices, passed_along(): lax.ppermute(value, axis, [(source, source + steps) for source in range(f...  21.7 us
    another operation x2, other arithmetic, per_device(): fields = jnp.stack(points, axis=0)  14 us
    slice x3, local copies, waits for them, and re-layouts, prefix_by_axis(): running = combine(running, jax.tree.map(lambda part: part[k], pieces))  13.8 us
    all_to_all x2, starting transfers between devices, moved(): lax.all_to_all(group, axis, split_axis=split_dim, concat_axis=concat_dim,...  12.4 us
    slice x3, local copies, waits for them, and re-layouts, grouped_exchange(): lax.slice_in_dim(a, low, high, axis=item_dim)  11 us
  transfers between devices with their start and end apart: 9, of which 8 were waited for; matrix products, arithmetic and copies ran while one was open for 13% of the time, Pallas kernels for 0%

commit v1 on v0

v1 whole, which is shorter than its diff:
```python
import jax
import jax.numpy as jnp
import numpy as np
from jax import lax
from jax.experimental import pallas as pl
from jax.experimental.pallas import tpu as pltpu
from jax.sharding import PartitionSpec as P

MESH = pl.DeviceIdType.MESH
F32, BF16 = jnp.float32, jnp.bfloat16
N = 128
SPACE = 8
TM = 32
STEPS = 4
TIME_STEP = 0.5
HALVES = 2
PAIRS = 4


def split_parts(table):
    high = table.astype(BF16)
    return high, (table - high.astype(np.float64)).astype(BF16)


def sine_table(length):
    ladder = np.arange(1, length + 1, dtype=np.float64)
    return np.sqrt(2.0 / (length + 1)) * np.sin(np.pi * ladder[:, None] * ladder[None, :] / (length + 1))


def eigen_values(length):
    ladder = np.arange(1, length + 1, dtype=np.float64)
    return -4.0 * np.sin(np.pi * ladder / (2 * (length + 1))) ** 2


def left_table(rows):
    high, low = split_parts(rows)
    return np.concatenate(
        [np.concatenate([high, high], axis=-1), np.concatenate([low, low], axis=-1)], axis=-2
    )


def tables():
    sine = sine_table(N)
    left = left_table(sine)
    right = np.ascontiguousarray(left.T)
    chosen = sine.reshape(SPACE, HALVES, PAIRS, 2, N).transpose(2, 0, 1, 3, 4).reshape(PAIRS, 32, N)
    anchor_y = left_table(chosen)
    anchor_x = left_table(sine.reshape(8, 16, N))
    line = eigen_values(N)
    plane = np.tile(line[:, None] + line[None, :], (1, 2)).astype(np.float32)
    along_y = np.repeat(line.reshape(SPACE, 8, 2), N, axis=2).astype(np.float32)
    return right, left, anchor_y, anchor_x, plane, along_y


def two_parts(value, axis):
    high = value.astype(BF16)
    low = (value - high.astype(F32)).astype(BF16)
    return jnp.concatenate([high, low], axis=axis)


def along_rows(value, right_ref):
    made = jnp.dot(two_parts(value, 1), right_ref[...], preferred_element_type=F32)
    return made[:, :N] + made[:, N:]


def along_columns(left, value):
    made = jnp.dot(left, two_parts(value, 0), preferred_element_type=F32)
    half = made.shape[0] // 2
    return made[:half] + made[half:]


def kernel(
    forcing_ref, guess_ref, initial_ref, right_ref, left_ref, anchor_y_ref, anchor_x_ref, plane_ref, along_y_ref,
    solution_ref, residual_ref,
    cells, first_cells, sent, received, anchor_rows, anchor_sent, anchor_received, anchor,
    fine, weight, coarse, guess, begin, parts, change, change_before, scan_in, scan_out, error_before,
    back_sent, back_received, made, residual,
    load_sem, store_sem, x_send, x_recv, anchor_send, anchor_recv, shift_send, shift_recv,
    scan_send, scan_recv, error_send, error_recv, back_send, back_recv,
):
    t, s = lax.axis_index("tm"), lax.axis_index("space")
    after = lax.rem(t + 1, TM)

    loads = [pltpu.make_async_copy(guess_ref.at[0], cells.at[0], load_sem.at[0])]
    loads += [pltpu.make_async_copy(forcing_ref.at[k], cells.at[k + 1], load_sem.at[k + 1]) for k in range(STEPS)]
    loads += [pltpu.make_async_copy(initial_ref, first_cells, load_sem.at[5])]
    for load in loads:
        load.start()

    barrier = pltpu.get_barrier_semaphore()
    for k in range(1, SPACE):
        pl.semaphore_signal(barrier, inc=1, device_id=(t, lax.rem(s + k, SPACE)), device_id_type=MESH)

    @pl.loop(1, TM)
    def _(k):
        pl.semaphore_signal(barrier, inc=1, device_id=(lax.rem(t + k, TM), s), device_id_type=MESH)

    def remote(src, dst, send, recv, tm, space):
        return pltpu.make_async_remote_copy(
            src_ref=src, dst_ref=dst, send_sem=send, recv_sem=recv, device_id=(tm, space), device_id_type=MESH
        )

    def arrived(like, send, recv):
        remote(like, like, send, recv, after, s).wait_recv()

    def left_here(like, send, recv):
        remote(like, like, send, recv, after, s).wait_send()

    def to_modes(field):
        @pl.loop(0, 4)
        def _(i):
            block = cells[field, pl.ds(4 * i, 4)].reshape(4 * N, N)
            block = along_rows(block, right_ref)
            for pair in range(2):
                both = jnp.concatenate([block[(2 * pair + u) * N : (2 * pair + u + 1) * N] for u in range(2)], axis=1)
                both = along_columns(left_ref[...], both)
                for u in range(2):
                    one = both[:, u * N : (u + 1) * N].reshape(SPACE, HALVES, 8, N)
                    x = 4 * i + 2 * pair + u
                    for h in range(HALVES):
                        sent[2 * field + h, :, pl.ds(pl.multiple_of(8 * x, 8), 8), :] = one[:, h]

    def exchange(field, h):
        at = 2 * field + h
        for k in range(1, SPACE):
            other = lax.rem(s + k, SPACE)
            remote(
                sent.at[at, other], received.at[at, pl.ds(pl.multiple_of(s * N, N), N)],
                x_send.at[at], x_recv.at[at], t, other,
            ).start()
        received[at, pl.ds(pl.multiple_of(s * N, N), N), :] = sent[at, s]

    loads[0].wait()
    to_modes(0)
    pl.semaphore_wait(barrier, SPACE - 1 + TM - 1)
    exchange(0, 0)
    exchange(0, 1)
    for field in range(1, STEPS + 1):
        loads[field].wait()
        to_modes(field)
        exchange(field, 0)
    for field in range(1, STEPS + 1):
        exchange(field, 1)

    loads[5].wait()
    column, block_of = lax.div(t, 8), lax.rem(t, 8)

    @pl.loop(0, 4)
    def _(i):
        for pair in range(2):
            both = jnp.concatenate([first_cells[4 * i + 2 * pair + u] for u in range(2)], axis=1)
            both = along_columns(anchor_y_ref[column], both)
            for u in range(2):
                x = 4 * i + 2 * pair + u
                anchor_rows[pl.ds(pl.multiple_of(32 * x, 32), 32), :] = both[:, u * N : (u + 1) * N]

    anchor_rows[...] = along_rows(anchor_rows[...], right_ref)
    for k in range(32):
        anchor_sent[k // 4, pl.ds(16 * (k % 4), 16), :] = anchor_rows[pl.ds(k, 16, stride=32), :]
    for k in range(1, SPACE):
        other = lax.rem(s + k, SPACE)
        remote(anchor_sent.at[other], anchor_received.at[s], anchor_send, anchor_recv, t, other).start()
    anchor_received[s] = anchor_sent[s]

    @pl.loop(0, HALVES * PAIRS)
    def _(i):
        spectrum = plane_ref[...] + along_y_ref[s, pl.ds(i, 1), :]
        inverse = 1.0 / (1.0 - 0.5 * TIME_STEP * spectrum)
        h, pair = lax.div(i, PAIRS), lax.rem(i, PAIRS)
        fine[h, pair] = (1.0 + 0.5 * TIME_STEP * spectrum) * inverse
        weight[h, pair] = TIME_STEP * inverse
        wide = 0.5 * STEPS * TIME_STEP
        coarse[h, pair] = (1.0 + wide * spectrum) / (1.0 - wide * spectrum)

    def lines(at, pair):
        return jnp.concatenate(
            [received[at, pl.ds(2 * pair + u, N, stride=8), :] for u in range(2)], axis=1
        )

    for h in range(HALVES):
        arrived(received.at[h, pl.ds(0, 7 * N)], x_send.at[h], x_recv.at[h])

        @pl.loop(0, PAIRS)
        def _(pair):
            guess[h, pair] = along_columns(left_ref[...], lines(h, pair))

        remote(guess.at[h], begin.at[h], shift_send.at[h], shift_recv.at[h], after, s).start()

    def relax(h):
        for field in range(1, STEPS + 1):
            at = 2 * field + h
            arrived(received.at[at, pl.ds(0, 7 * N)], x_send.at[at], x_recv.at[at])

            @pl.loop(0, PAIRS)
            def _(pair):
                source = along_columns(left_ref[...], lines(at, pair)) * weight[h, pair]
                if field > 1:
                    source = source + fine[h, pair] * parts[field - 2, h, pair]
                parts[field - 1, h, pair] = source

        arrived(begin.at[h], shift_send.at[h], shift_recv.at[h])

        @pl.loop(0, PAIRS)
        def _(pair):
            square = fine[h, pair] * fine[h, pair]
            value = square * square * begin[h, pair] + parts[3, h, pair]
            parts[3, h, pair] = value
            known = guess[h, pair]
            change[h, pair] = jnp.where(t == TM - 1, known, value - known)

        @pl.loop(1, TM)
        def _(k):
            other = lax.rem(t + k, TM)
            rows = pl.ds(pl.multiple_of(16 * lax.rem(other, 8), 16), 16)
            remote(
                change.at[h, lax.div(other, 8), rows], scan_in.at[h, t], scan_send.at[h], scan_recv.at[h], other, s
            ).start()

        mine = pl.ds(pl.multiple_of(16 * block_of, 16), 16)
        scan_in[h, t] = change[h, column, mine, :]
        remote(change.at[h], change_before.at[h], shift_send.at[2 + h], shift_recv.at[2 + h], after, s).start()

    def scan(h):
        arrived(scan_in.at[h, pl.ds(0, TM - 1)], scan_send.at[h], scan_recv.at[h])
        mine = pl.ds(pl.multiple_of(16 * block_of, 16), 16)
        square = fine[h, column, mine, :] * fine[h, column, mine, :]
        power, rate = square * square, coarse[h, column, mine, :]
        first = anchor[h] - scan_in[h, TM - 1]
        scan_out[h, 0] = first

        def sweep(j, error):
            scan_out[h, j] = error
            return rate * error + power * scan_in[h, j - 1]

        scan_out[h, TM - 1] = lax.fori_loop(1, TM - 1, sweep, power * first)

        @pl.loop(1, TM)
        def _(k):
            other = lax.rem(t + k, TM)
            remote(
                scan_out.at[h, other], error_before.at[h, column, mine], error_send.at[h], error_recv.at[h], other, s
            ).start()

        error_before[h, column, mine, :] = scan_out[h, t]

    def go_back(h):
        arrived(change_before.at[h], shift_send.at[2 + h], shift_recv.at[2 + h])
        arrived(scan_out.at[h, pl.ds(0, TM - 1)], error_send.at[h], error_recv.at[h])

        @pl.loop(0, PAIRS)
        def _(pair):
            came = error_before[h, pair]
            delta = jnp.where(t == 0, came, change_before[h, pair])
            error = jnp.where(t == 0, jnp.zeros_like(came), came)
            rate = fine[h, pair]
            square = rate * rate
            gap = square * square * delta
            for u in range(2):
                residual[pl.ds(8 * h + 2 * pair + u, N, stride=16), :] = gap[:, u * N : (u + 1) * N]
            third = begin[h, pair] + (delta + error)
            for k in range(STEPS):
                if k == 0:
                    point = rate * third + parts[0, h, pair]
                elif k == 1:
                    point = square * third + parts[1, h, pair]
                elif k == 2:
                    point = rate * square * third + parts[2, h, pair]
                else:
                    point = parts[3, h, pair] + (gap + coarse[h, pair] * error)
                point = along_columns(left_ref[...], point)
                for u in range(2):
                    rows = pl.ds(pl.multiple_of(32 * pair + 16 * u, 16), 16)
                    back_sent[2 * k + h, :, rows, :] = point[:, u * N : (u + 1) * N].reshape(SPACE, 16, N)

        for k in range(STEPS):
            at = 2 * k + h
            slot = pl.ds(pl.multiple_of(256 * s + 128 * h, 128), 128)
            for hop in range(1, SPACE):
                other = lax.rem(s + hop, SPACE)
                remote(
                    back_sent.at[at, other], back_received.at[k, slot], back_send.at[at], back_recv.at[at], t, other
                ).start()
            back_received[k, slot, :] = back_sent[at, s]

    relax(0)
    arrived(anchor_received.at[pl.ds(0, SPACE - 1)], anchor_send, anchor_recv)
    for h in range(HALVES):
        both = jnp.concatenate(
            [anchor_received[:, pl.ds(32 * h + 16 * u, 16), :].reshape(N, N) for u in range(2)], axis=1
        )
        anchor[h] = along_columns(anchor_x_ref[block_of], both)
    scan(0)
    relax(1)
    go_back(0)
    scan(1)
    go_back(1)
    pltpu.make_async_copy(residual, residual_ref, store_sem.at[STEPS]).start()

    stores = []
    for k in range(STEPS):
        for h in range(HALVES):
            at = 2 * k + h
            arrived(back_received.at[k, pl.ds(0, 7 * N)], back_send.at[at], back_recv.at[at])

        @pl.loop(0, 4)
        def _(i):
            pieces = []
            for pair in range(2):
                x = 4 * i + 2 * pair
                both = jnp.concatenate(
                    [back_received[k, pl.ds(x + u, N, stride=16), :] for u in range(2)], axis=1
                )
                both = along_columns(left_ref[...], both)
                pieces += [both[:, :N], both[:, N:]]
            block = along_rows(jnp.concatenate(pieces, axis=0), right_ref)
            made[k, pl.ds(4 * i, 4)] = block.reshape(4, N, N)

        stores.append(pltpu.make_async_copy(made.at[k], solution_ref.at[k], store_sem.at[k]))
        stores[-1].start()

    for at in range(2 * (STEPS + 1)):
        left_here(received.at[at, pl.ds(0, 7 * N)], x_send.at[at], x_recv.at[at])
    left_here(anchor_received.at[pl.ds(0, SPACE - 1)], anchor_send, anchor_recv)
    for h in range(HALVES):
        left_here(guess.at[h], shift_send.at[h], shift_recv.at[h])
        left_here(change.at[h], shift_send.at[2 + h], shift_recv.at[2 + h])
        left_here(scan_in.at[h, pl.ds(0, TM - 1)], scan_send.at[h], scan_recv.at[h])
        left_here(scan_out.at[h, pl.ds(0, TM - 1)], error_send.at[h], error_recv.at[h])
    for at in range(2 * STEPS):
        left_here(back_received.at[0, pl.ds(0, 7 * N)], back_send.at[at], back_recv.at[at])
    for store in stores:
        store.wait()
    pltpu.make_async_copy(residual, residual_ref, store_sem.at[STEPS]).wait()


def per_device(forcing, coarse_guess, initial):
    modal = (HALVES, PAIRS, N, 2 * N)
    dma = pltpu.SemaphoreType.DMA
    vmem = pl.BlockSpec(memory_space=pltpu.VMEM)
    anywhere = pl.BlockSpec(memory_space=pl.ANY)
    given = tables()
    out, gap = pl.pallas_call(
        kernel,
        out_shape=(
            jax.ShapeDtypeStruct((STEPS, 16, N, N), F32),
            jax.ShapeDtypeStruct((16 * N, N), F32),
        ),
        in_specs=[anywhere] * 3 + [vmem] * len(given),
        out_specs=(anywhere, anywhere),
        scratch_shapes=[
            pltpu.VMEM((STEPS + 1, 16, N, N), F32),
            pltpu.VMEM((16, N, N), F32),
            pltpu.VMEM((2 * (STEPS + 1), SPACE, N, N), F32),
            pltpu.VMEM((2 * (STEPS + 1), SPACE * N, N), F32),
            pltpu.VMEM((512, N), F32),
            pltpu.VMEM((SPACE, 64, N), F32),
            pltpu.VMEM((SPACE, 64, N), F32),
            pltpu.VMEM((HALVES, 16, 2 * N), F32),
            pltpu.VMEM(modal, F32),
            pltpu.VMEM(modal, F32),
            pltpu.VMEM(modal, F32),
            pltpu.VMEM(modal, F32),
            pltpu.VMEM(modal, F32),
            pltpu.VMEM((STEPS,) + modal, F32),
            pltpu.VMEM(modal, F32),
            pltpu.VMEM(modal, F32),
            pltpu.VMEM((HALVES, TM, 16, 2 * N), F32),
            pltpu.VMEM((HALVES, TM, 16, 2 * N), F32),
            pltpu.VMEM(modal, F32),
            pltpu.VMEM((2 * STEPS, SPACE, N, N), F32),
            pltpu.VMEM((STEPS, 16 * N, N), F32),
            pltpu.VMEM((STEPS, 16, N, N), F32),
            pltpu.VMEM((16 * N, N), F32),
            dma((STEPS + 2,)),
            dma((STEPS + 1,)),
            dma((2 * (STEPS + 1),)),
            dma((2 * (STEPS + 1),)),
            dma,
            dma,
            dma((4,)),
            dma((4,)),
            dma((HALVES,)),
            dma((HALVES,)),
            dma((HALVES,)),
            dma((HALVES,)),
            dma((2 * STEPS,)),
            dma((2 * STEPS,)),
        ],
        compiler_params=pltpu.CompilerParams(
            collective_id=0, has_side_effects=True, vmem_limit_bytes=62 * 1024 * 1024
        ),
    )(forcing, coarse_guess, initial, *given)
    return out, gap.reshape(1, N, 16, N)


def solution(mesh):
    in_specs = (P("tm", "space", None, None), P("tm", "space", None, None), P("space", None, None))
    out_specs = (P("tm", "space", None, None), P("tm", None, "space", None))
    return jax.shard_map(per_device, mesh=mesh, in_specs=in_specs, out_specs=out_specs, check_vma=False)
```

time: 481 us -> 158 us (0.33); the launches traced: 471 us -> 158 us
  waiting for transfers between devices: 324 us -> 0 us
  Pallas kernels: 0 us -> 151 us
  local copies, waits for them, and re-layouts: 44 us -> 5.76 us
  matrix products: 34.6 us -> 0 us
  other arithmetic: 33.4 us -> 0 us
  starting transfers between devices: 20.7 us -> 0 us
  between operations: 14.2 us -> 0.65 us
    all_gather x4 -> x0, waiting for transfers between devices: 183 us -> none  [prefix_by_axis(): pieces = jax.tree.map(lambda part: lax.all_gather(part, axis), running)]
    pallas_call x0 -> x1, Pallas kernels: none -> 151 us  [per_device(): pl.pallas_call(kernel, out_shape=(jax.ShapeDtypeStruct((STEPS, 16, N, N),...]
    all_to_all x3 -> x0, waiting for transfers between devices: 111 us -> none  [the longest x2 63.4 us: moved(): lax.all_to_all(group, axis, split_axis=split_dim, concat_axis=concat_dim,...]
    dot_general x7 -> x0, matrix products: 34.6 us -> none  [the longest x1 8.01 us: per_device(): fields = jnp.einsum('bxyz,zr->bxyr', fields, table_z, precision=highest)]
    ppermute x2 -> x0, waiting for transfers between devices: 30.9 us -> none  [the longest x1 21.7 us: passed_along(): lax.ppermute(value, axis, [(source, source + steps) for source in range(f...]
    slice x6 -> x0, local copies, waits for them, and re-layouts: 24.8 us -> none  [the longest x3 13.8 us: prefix_by_axis(): running = combine(running, jax.tree.map(lambda part: part[k], pieces))]
    all_to_all x3 -> x0, starting transfers between devices: 18.1 us -> none  [the longest x2 12.4 us: moved(): lax.all_to_all(group, axis, split_axis=split_dim, concat_axis=concat_dim,...]
    another operation x2 -> x0, other arithmetic: 14 us -> none  [per_device(): fields = jnp.stack(points, axis=0)]
  transfers between devices with their start and end apart: 9 -> 0, of which waited for: 8 -> 0; matrix products, arithmetic and copies ran while one was open for 13% -> 0% of each run, Pallas kernels for 0% -> 0%
where the time goes in v1:
time: 158 us
  Pallas kernels  151 us (96%)
  local copies, waits for them, and re-layouts  5.76 us (4%)
    pallas_call x1, Pallas kernels, per_device(): pl.pallas_call(kernel, out_shape=(jax.ShapeDtypeStruct((STEPS, 16, N, N),...  151 us
    unnamed x4, local copies, waits for them, and re-layouts  5.76 us

profile of v1, /device:TPU:1, one launch (start us, length us, event | category | flops | bytes accessed | tf_op | source)
XLA Modules:
  0.0 157.8 jit_solution(12572800436560055299)
XLA Ops:
  0.6 151.4 %shard_map.104 = (f32[4,16,128,128]{3,2,1,0:T(8,128)}, f32[2048,128]{1,0:T(8,128)}) custom-call(f32[4,16,128,128]{3,2,1,0:T(8,128)} %forcing_ref.1, f32[1,16,128,128]{3,2,1,0:T(8,128)} %guess_ref.1, f32[16,128,128]{2,1,0:T(8,128)} %initial_ref.1, bf16[256,256]{1,0:T(8,128)(2,1)} %constant.12.clone.right_ref, bf16[256,256]{1,0:T(8,128)(2,1)} %constant.13.clone.left_ref, ...), custom_call_target="tpu_custom_call" | custom-call | tf_op jit(solution)/shard_map/pallas_call | solution.py:342
  152.0 0.0 copy-start
  152.1 4.8 %copy.13 = f32[4,16,128,128]{3,2,1,0:T(8,128)} copy(f32[4,16,128,128]{3,2,1,0:T(8,128)} %get-tuple-element.8) | data formatting | bytes 8388608
  156.8 0.0 copy-done
  156.8 1.0 copy.14
Async XLA Ops:
  152.0 4.8 %copy-start = (f32[2048,128]{1,0:T(8,128)S(1)}, f32[2048,128]{1,0:T(8,128)}, u32[]{:S(2)}) copy-start(f32[2048,128]{1,0:T(8,128)} %get-tuple-element.5) | copy-start | bytes 3145732

commit v2 on v1

v2 whole, which is shorter than its diff:
```python
import jax
import jax.numpy as jnp
import numpy as np
from jax import lax
from jax.experimental import pallas as pl
from jax.experimental.pallas import tpu as pltpu
from jax.sharding import PartitionSpec as P

MESH = pl.DeviceIdType.MESH
F32, BF16 = jnp.float32, jnp.bfloat16
N = 128
SPACE = 8
TM = 32
STEPS = 4
TIME_STEP = 0.5
HALVES = 2
PAIRS = 4
CHUNKS = 2
GROUP = PAIRS // CHUNKS
ROWS = N * GROUP // TM
FIELDS = 4
BACK = 3
HALF_STEP = 0.5 * TIME_STEP


def split_parts(table):
    high = table.astype(BF16)
    return high, (table - high.astype(np.float64)).astype(BF16)


def sine_table(length):
    ladder = np.arange(1, length + 1, dtype=np.float64)
    return np.sqrt(2.0 / (length + 1)) * np.sin(np.pi * ladder[:, None] * ladder[None, :] / (length + 1))


def eigen_values(length):
    ladder = np.arange(1, length + 1, dtype=np.float64)
    return -4.0 * np.sin(np.pi * ladder / (2 * (length + 1))) ** 2


def left_table(rows):
    high, low = split_parts(rows)
    return np.concatenate(
        [np.concatenate([high, high], axis=-1), np.concatenate([low, low], axis=-1)], axis=-2
    )


def tables():
    sine = sine_table(N)
    left = left_table(sine)
    right = np.ascontiguousarray(left.T)
    chosen = sine.reshape(SPACE, HALVES, CHUNKS, GROUP, 2, N).transpose(3, 0, 1, 2, 4, 5).reshape(GROUP, 64, N)
    anchor_y = left_table(chosen)
    anchor_x = left_table(sine.reshape(N // ROWS, ROWS, N))
    beside = np.zeros((2, SPACE, N))
    beside[0, 1:] = sine[15:-1:16]
    beside[1, :-1] = sine[16::16]
    beside = left_table(beside.reshape(16, N))
    line = eigen_values(N)
    plane = np.tile(line[:, None] + line[None, :], (1, 2)).astype(np.float32)
    along_y = np.repeat(line.reshape(SPACE, 8, 2), N, axis=2).astype(np.float32)
    return right, left, anchor_y, anchor_x, beside, plane, along_y


def two_parts(value, axis):
    high = value.astype(BF16)
    low = (value - high.astype(F32)).astype(BF16)
    return jnp.concatenate([high, low], axis=axis)


def along_rows(value, right_ref):
    made = jnp.dot(two_parts(value, 1), right_ref[...], preferred_element_type=F32)
    return made[:, :N] + made[:, N:]


def along_columns(left, value):
    made = jnp.dot(left, two_parts(value, 0), preferred_element_type=F32)
    half = made.shape[0] // 2
    return made[:half] + made[half:]


def kernel(
    forcing_ref, guess_ref, initial_ref, *refs,
):
    given, (
    solution_ref, residual_ref,
    cells, first_cells, gap_cells, sent, received, anchor_rows, anchor_sent, anchor_received, anchor,
    fine, weight, coarse, guess, begin, parts, change, change_before, scan_in, scan_out, error_before,
    back_sent, back_received, beside_sent, beside_received, beside_cells,
    load_sem, x_send, x_recv, plane_send, plane_recv, anchor_send, anchor_recv, shift_send, shift_recv,
    change_send, change_recv, scan_send, scan_recv, error_send, error_recv, back_send, back_recv,
    beside_send, beside_recv,
    table_sem, right_ref, left_ref, anchor_y_ref, anchor_x_ref, beside_ref, plane_ref, along_y_ref,
    ) = refs[:7], refs[7:]
    tables_here = (right_ref, left_ref, anchor_y_ref, anchor_x_ref, beside_ref, plane_ref, along_y_ref)
    t, s = lax.axis_index("tm"), lax.axis_index("space")
    after = lax.rem(t + 1, TM)
    right_of, left_of = lax.rem(s + 1, SPACE), lax.rem(s + SPACE - 1, SPACE)

    barrier = pltpu.get_barrier_semaphore()

    @pl.loop(0, TM - 1)
    def _(k):
        far = 1 + lax.rem(k + 15, TM - 1)
        pl.semaphore_signal(barrier, inc=1, device_id=(lax.rem(t + far, TM), s), device_id_type=MESH)

    for k in range(1, SPACE):
        pl.semaphore_signal(barrier, inc=1, device_id=(t, lax.rem(s + k, SPACE)), device_id_type=MESH)

    loads = [pltpu.make_async_copy(guess_ref.at[0], cells.at[0], load_sem.at[0])]
    loads += [pltpu.make_async_copy(forcing_ref.at[k], cells.at[k + 1], load_sem.at[k + 1]) for k in range(STEPS)]
    loads += [pltpu.make_async_copy(initial_ref, first_cells, load_sem.at[5])]
    loads[0].start()
    table_loads = [
        pltpu.make_async_copy(src, dst, table_sem.at[k]) for k, (src, dst) in enumerate(zip(given, tables_here))
    ]
    for load in table_loads[:2] + loads[1:] + table_loads[2:]:
        load.start()

    def remote(src, dst, send, recv, tm, space):
        return pltpu.make_async_remote_copy(
            src_ref=src, dst_ref=dst, send_sem=send, recv_sem=recv, device_id=(tm, space), device_id_type=MESH
        )

    def arrived(like, send, recv):
        remote(like, like, send, recv, after, s).wait_recv()

    def left_here(like, send, recv):
        remote(like, like, send, recv, after, s).wait_send()

    def over_columns(block):
        for pair in range(2):
            both = jnp.concatenate([block[(2 * pair + u) * N : (2 * pair + u + 1) * N] for u in range(2)], axis=1)
            yield pair, along_columns(left_ref[...], both)

    def put(slot, first, both):
        for u in range(2):
            one = both[:, u * N : (u + 1) * N].reshape(SPACE, HALVES, 8, N)
            for h in range(HALVES):
                sent[2 * slot + h, :, pl.ds(pl.multiple_of(8 * (first + u), 8), 8), :] = one[:, h]

    def to_modes(field, slot):
        @pl.loop(0, 4, unroll=True)
        def _(i):
            block = along_rows(cells[field, pl.ds(4 * i, 4)].reshape(4 * N, N), right_ref)
            for pair, both in over_columns(block):
                put(slot, 4 * i + 2 * pair, both)

    def middle_to_modes(slot):
        @pl.loop(0, 4, unroll=True)
        def _(i):
            here = gap_cells[pl.ds(4 * i + 1, 4)]
            bent = gap_cells[pl.ds(4 * i, 4)] + gap_cells[pl.ds(4 * i + 2, 4)] - 2.0 * here
            total = cells[2, pl.ds(4 * i, 4)] + cells[3, pl.ds(4 * i, 4)] + HALF_STEP * bent
            total = along_rows(total.reshape(4 * N, N), right_ref)
            here = along_rows(here.reshape(4 * N, N), right_ref)
            for (pair, both), (_, more) in zip(over_columns(total), over_columns(here)):
                put(slot, 4 * i + 2 * pair, both + (HALF_STEP * plane_ref[...]) * more)

    def exchange(slot, h):
        at = 2 * slot + h
        for k in range(1, SPACE):
            other = lax.rem(s + k, SPACE)
            remote(
                sent.at[at, other], received.at[at, pl.ds(pl.multiple_of(s * N, N), N)],
                x_send.at[at], x_recv.at[at], t, other,
            ).start()
        received[at, pl.ds(pl.multiple_of(s * N, N), N), :] = sent[at, s]

    def lines(at, pair):
        return jnp.concatenate(
            [received[at, pl.ds(2 * pair + u, N, stride=8), :] for u in range(2)], axis=1
        )

    def whole_lines(at):
        arrived(received.at[at, pl.ds(0, 7 * N)], x_send.at[at], x_recv.at[at])

    def pass_guess(h):
        whole_lines(h)
        for pair in range(PAIRS):
            guess[h, pair] = along_columns(left_ref[...], lines(h, pair))
        remote(guess.at[h], begin.at[h], shift_send.at[h], shift_recv.at[h], after, s).start()

    loads[0].wait()
    for load in table_loads:
        load.wait()
    to_modes(0, 0)
    loads[2].wait()
    loads[3].wait()
    gap_cells[pl.ds(1, 16)] = cells[2] - cells[3]
    pl.semaphore_wait(barrier, SPACE - 1 + TM - 1)
    exchange(0, 0)
    exchange(0, 1)
    planes = [
        remote(gap_cells.at[16], gap_cells.at[0], plane_send.at[0], plane_recv.at[0], t, right_of),
        remote(gap_cells.at[1], gap_cells.at[17], plane_send.at[1], plane_recv.at[1], t, left_of),
    ]
    for plane in planes:
        plane.start()
    loads[1].wait()
    to_modes(1, 1)
    exchange(1, 0)
    loads[4].wait()
    to_modes(4, 2)
    exchange(2, 0)
    pass_guess(0)
    for plane in planes:
        plane.wait_recv()
    gap_cells[0] = jnp.where(s == 0, jnp.zeros((N, N), F32), gap_cells[0])
    gap_cells[17] = jnp.where(s == SPACE - 1, jnp.zeros((N, N), F32), gap_cells[17])
    middle_to_modes(3)
    exchange(3, 0)
    pass_guess(1)

    loads[5].wait()
    column, block_of = lax.div(t, TM // GROUP), lax.rem(t, TM // GROUP)
    mine = pl.ds(pl.multiple_of(ROWS * block_of, ROWS), ROWS)

    @pl.loop(0, 4, unroll=True)
    def _(i):
        for pair in range(2):
            both = jnp.concatenate([first_cells[4 * i + 2 * pair + u] for u in range(2)], axis=1)
            both = along_columns(anchor_y_ref[column], both)
            both = jnp.concatenate([both[:, :N], both[:, N:]], axis=0)
            both = along_rows(both, right_ref)
            anchor_rows[pl.ds(pl.multiple_of(256 * i + 128 * pair, 128), 128), :] = both

    @pl.loop(0, SPACE)
    def _(other):
        for k in range(8):
            anchor_sent[other, pl.ds(16 * k, 16), :] = anchor_rows[pl.ds(8 * other + k, 16, stride=64), :]

    for k in range(1, SPACE):
        other = lax.rem(s + k, SPACE)
        remote(anchor_sent.at[other], anchor_received.at[s], anchor_send, anchor_recv, t, other).start()
    anchor_received[s] = anchor_sent[s]
    for slot in range(1, FIELDS):
        exchange(slot, 1)

    @pl.loop(0, HALVES * PAIRS)
    def _(i):
        spectrum = plane_ref[...] + along_y_ref[s, pl.ds(i, 1), :]
        inverse = 1.0 / (1.0 - HALF_STEP * spectrum)
        h, pair = lax.div(i, PAIRS), lax.rem(i, PAIRS)
        fine[h, pair] = (1.0 + HALF_STEP * spectrum) * inverse
        weight[h, pair] = TIME_STEP * inverse
        wide = STEPS * HALF_STEP
        coarse[h, pair] = (1.0 + wide * spectrum) / (1.0 - wide * spectrum)

    def pass_change(h, c):
        at, pairs = CHUNKS * h + c, pl.ds(GROUP * c, GROUP)
        remote(
            change.at[h, pairs], change_before.at[h, pairs], change_send.at[at], change_recv.at[at], after, s
        ).start()

    def relax(h):
        whole_lines(2 + h)

        @pl.loop(0, PAIRS, unroll=True)
        def _(pair):
            parts[0, h, pair] = along_columns(left_ref[...], lines(2 + h, pair)) * weight[h, pair]

        whole_lines(4 + h)

        @pl.loop(0, PAIRS, unroll=True)
        def _(pair):
            parts[2, h, pair] = along_columns(left_ref[...], lines(4 + h, pair)) * weight[h, pair]

        whole_lines(6 + h)
        arrived(begin.at[h], shift_send.at[h], shift_recv.at[h])
        for c in range(CHUNKS):

            @pl.loop(GROUP * c, GROUP * (c + 1), unroll=True)
            def _(pair):
                rate, scale = fine[h, pair], weight[h, pair]
                square = rate * rate
                third = along_columns(left_ref[...], lines(6 + h, pair)) * (scale * scale * (1.0 / TIME_STEP))
                third = third + square * parts[0, h, pair]
                parts[1, h, pair] = third
                value = parts[2, h, pair] + rate * third
                value = square * square * begin[h, pair] + value
                parts[2, h, pair] = value
                known = guess[h, pair]
                change[h, pair] = jnp.where(t == TM - 1, known, value - known)

            at = CHUNKS * h + c

            @pl.loop(0, TM - 1)
            def _(k):
                far = 1 + lax.rem(k + 15, TM - 1)
                other = lax.rem(t + far, TM)
                rows = pl.ds(pl.multiple_of(ROWS * lax.rem(other, TM // GROUP), ROWS), ROWS)
                remote(
                    change.at[h, GROUP * c + lax.div(other, TM // GROUP), rows], scan_in.at[at, t],
                    scan_send.at[at], scan_recv.at[at], other, s,
                ).start()

            scan_in[at, t] = change[h, GROUP * c + column, mine, :]
        pass_change(h, 0)

    def scan(h, c):
        at = CHUNKS * h + c
        arrived(scan_in.at[at, pl.ds(0, TM - 1)], scan_send.at[at], scan_recv.at[at])
        one = fine[h, GROUP * c + column, mine, :]
        square = one * one
        power, rate = square * square, coarse[h, GROUP * c + column, mine, :]
        first = anchor[at] - scan_in[at, TM - 1]
        scan_out[at, 0] = first

        def sweep(j, error):
            scan_out[at, j] = error
            return rate * error + power * scan_in[at, j - 1]

        scan_out[at, TM - 1] = lax.fori_loop(1, TM - 1, sweep, power * first)

        @pl.loop(0, TM - 1)
        def _(k):
            far = 1 + lax.rem(k + 15, TM - 1)
            other = lax.rem(t + far, TM)
            remote(
                scan_out.at[at, other], error_before.at[h, GROUP * c + column, mine],
                error_send.at[at], error_recv.at[at], other, s,
            ).start()

        error_before[h, GROUP * c + column, mine, :] = scan_out[at, t]

    def go_back(h, c):
        at, pairs = CHUNKS * h + c, pl.ds(GROUP * c, GROUP)
        arrived(change_before.at[h, pairs], change_send.at[at], change_recv.at[at])
        arrived(scan_out.at[at, pl.ds(0, TM - 1)], error_send.at[at], error_recv.at[at])

        @pl.loop(0, GROUP, unroll=True)
        def _(i):
            pair = GROUP * c + i
            came = error_before[h, pair]
            delta = jnp.where(t == 0, came, change_before[h, pair])
            error = jnp.where(t == 0, jnp.zeros_like(came), came)
            rate = fine[h, pair]
            square = rate * rate
            gap = square * square * delta
            for u in range(2):
                residual_ref[pl.ds(8 * h + 2 * pair + u, N, stride=16), :] = gap[:, u * N : (u + 1) * N]
            start = begin[h, pair] + (delta + error)
            first = rate * start + parts[0, h, pair]
            third = rate * square * start + parts[1, h, pair]
            last = parts[2, h, pair] + (gap + coarse[h, pair] * error)
            for k, point in enumerate((first, third, last)):
                point = along_columns(left_ref[...], point)
                for u in range(2):
                    rows = pl.ds(pl.multiple_of(32 * i + 16 * u, 16), 16)
                    back_sent[4 * k + at, :, rows, :] = point[:, u * N : (u + 1) * N].reshape(SPACE, 16, N)
            point = along_columns(beside_ref[...], first - third)
            for u in range(2):
                for side in range(2):
                    rows = pl.ds(4 * i + 2 * u + side, 8, stride=8)
                    beside_sent[at, rows, :] = point[8 * side : 8 * side + 8, u * N : (u + 1) * N]

        for k in range(BACK):
            slot = pl.ds(pl.multiple_of(256 * s + 64 * at, 64), 64)
            for hop in range(1, SPACE):
                other = lax.rem(s + hop, SPACE)
                remote(
                    back_sent.at[4 * k + at, other], back_received.at[k, slot],
                    back_send.at[4 * k + at], back_recv.at[4 * k + at], t, other,
                ).start()
            back_received[k, slot, :] = back_sent[4 * k + at, s]
            if k == 1:
                slot = pl.ds(pl.multiple_of(32 * s + 8 * at, 8), 8)
                for hop in range(1, SPACE):
                    other = lax.rem(s + hop, SPACE)
                    remote(
                        beside_sent.at[at, pl.ds(pl.multiple_of(8 * other, 8), 8)], beside_received.at[slot],
                        beside_send.at[at], beside_recv.at[at], t, other,
                    ).start()
                beside_received[slot, :] = beside_sent[at, pl.ds(pl.multiple_of(8 * s, 8), 8), :]

    relax(0)
    arrived(anchor_received.at[pl.ds(0, SPACE - 1)], anchor_send, anchor_recv)
    for at in range(HALVES * CHUNKS):
        both = jnp.concatenate(
            [anchor_received[:, pl.ds(32 * at + 16 * u, 16), :].reshape(N, N) for u in range(2)], axis=1
        )
        anchor[at] = along_columns(anchor_x_ref[block_of], both)
    scan(0, 0)
    pass_change(0, 1)
    scan(0, 1)
    relax(1)
    go_back(0, 0)
    go_back(0, 1)
    scan(1, 0)
    pass_change(1, 1)
    scan(1, 1)
    go_back(1, 0)
    go_back(1, 1)
    def back(k):
        for at in range(HALVES * CHUNKS):
            arrived(back_received.at[k, pl.ds(0, 7 * 64)], back_send.at[4 * k + at], back_recv.at[4 * k + at])

    def columns_at(k, x):
        return jnp.concatenate([back_received[k, pl.ds(x + u, N, stride=16), :] for u in range(2)], axis=1)

    def to_cells(four):
        pieces = []
        for both in four:
            both = along_columns(left_ref[...], both)
            pieces += [both[:, :N], both[:, N:]]
        return along_rows(jnp.concatenate(pieces, axis=0), right_ref)

    for k, step in ((0, 0), (1, 2)):
        back(k)

        @pl.loop(0, 4, unroll=True)
        def _(i):
            block = to_cells([columns_at(k, 4 * i + 2 * pair) for pair in range(2)])
            solution_ref[step, pl.ds(4 * i, 4)] = block.reshape(4, N, N)


    for at in range(HALVES * CHUNKS):
        arrived(beside_received.at[pl.ds(0, 7 * 8)], beside_send.at[at], beside_recv.at[at])
    both = jnp.concatenate([beside_received[pl.ds(side, N, stride=2), :] for side in range(2)], axis=1)
    beside_cells[pl.ds(0, 2)] = to_cells([both]).reshape(2, N, N)

    @pl.loop(0, 16)
    def _(x):
        beside_cells[x + 2] = solution_ref[0, x] - solution_ref[2, x]

    beside_cells[18] = beside_cells[1]
    beside_cells[1] = beside_cells[0]

    @pl.loop(0, 4, unroll=True)
    def _(i):
        four = [
            (columns_at(0, 4 * i + 2 * pair) - columns_at(1, 4 * i + 2 * pair)) * plane_ref[...]
            for pair in range(2)
        ]
        block = to_cells(four).reshape(4, N, N)
        planes = pl.ds(4 * i, 4)
        bent = beside_cells[pl.ds(4 * i + 1, 4)] + beside_cells[pl.ds(4 * i + 3, 4)]
        bent = bent - 2.0 * beside_cells[pl.ds(4 * i + 2, 4)] + block
        total = solution_ref[0, planes] + solution_ref[2, planes] + HALF_STEP * bent
        solution_ref[1, planes] = 0.5 * total + HALF_STEP * gap_cells[pl.ds(4 * i + 1, 4)]

    back(2)

    @pl.loop(0, 4, unroll=True)
    def _(i):
        block = to_cells([columns_at(2, 4 * i + 2 * pair) for pair in range(2)])
        solution_ref[3, pl.ds(4 * i, 4)] = block.reshape(4, N, N)


    for at in range(2 * FIELDS):
        left_here(received.at[at, pl.ds(0, 7 * N)], x_send.at[at], x_recv.at[at])
    for plane in planes:
        plane.wait_send()
    left_here(anchor_received.at[pl.ds(0, SPACE - 1)], anchor_send, anchor_recv)
    for h in range(HALVES):
        left_here(guess.at[h], shift_send.at[h], shift_recv.at[h])
    for at in range(HALVES * CHUNKS):
        left_here(change.at[0, pl.ds(0, GROUP)], change_send.at[at], change_recv.at[at])
        left_here(scan_in.at[at, pl.ds(0, TM - 1)], scan_send.at[at], scan_recv.at[at])
        left_here(scan_out.at[at, pl.ds(0, TM - 1)], error_send.at[at], error_recv.at[at])
        left_here(beside_received.at[pl.ds(0, 7 * 8)], beside_send.at[at], beside_recv.at[at])
    for at in range(BACK * HALVES * CHUNKS):
        left_here(back_received.at[0, pl.ds(0, 7 * 64)], back_send.at[at], back_recv.at[at])


def per_device(forcing, coarse_guess, initial):
    modal = (HALVES, PAIRS, N, 2 * N)
    quarters = HALVES * CHUNKS
    dma = pltpu.SemaphoreType.DMA
    vmem = pl.BlockSpec(memory_space=pltpu.VMEM)
    anywhere = pl.BlockSpec(memory_space=pltpu.HBM)
    given = tuple(jnp.asarray(one) for one in tables())
    out, gap = pl.pallas_call(
        kernel,
        out_shape=(
            jax.ShapeDtypeStruct((STEPS, 16, N, N), F32),
            jax.ShapeDtypeStruct((16 * N, N), F32),
        ),
        in_specs=[anywhere] * (3 + len(given)),
        out_specs=(vmem, vmem),
        scratch_shapes=[
            pltpu.VMEM((STEPS + 1, 16, N, N), F32),
            pltpu.VMEM((16, N, N), F32),
            pltpu.VMEM((18, N, N), F32),
            pltpu.VMEM((2 * FIELDS, SPACE, N, N), F32),
            pltpu.VMEM((2 * FIELDS, SPACE * N, N), F32),
            pltpu.VMEM((1024, N), F32),
            pltpu.VMEM((SPACE, N, N), F32),
            pltpu.VMEM((SPACE, N, N), F32),
            pltpu.VMEM((quarters, ROWS, 2 * N), F32),
            pltpu.VMEM(modal, F32),
            pltpu.VMEM(modal, F32),
            pltpu.VMEM(modal, F32),
            pltpu.VMEM(modal, F32),
            pltpu.VMEM(modal, F32),
            pltpu.VMEM((3,) + modal, F32),
            pltpu.VMEM(modal, F32),
            pltpu.VMEM(modal, F32),
            pltpu.VMEM((quarters, TM, ROWS, 2 * N), F32),
            pltpu.VMEM((quarters, TM, ROWS, 2 * N), F32),
            pltpu.VMEM(modal, F32),
            pltpu.VMEM((BACK * quarters, SPACE, 64, N), F32),
            pltpu.VMEM((BACK, 16 * N, N), F32),
            pltpu.VMEM((quarters, 64, N), F32),
            pltpu.VMEM((2 * N, N), F32),
            pltpu.VMEM((19, N, N), F32),
            dma((STEPS + 2,)),
            dma((2 * FIELDS,)),
            dma((2 * FIELDS,)),
            dma((2,)),
            dma((2,)),
            dma,
            dma,
            dma((HALVES,)),
            dma((HALVES,)),
            dma((quarters,)),
            dma((quarters,)),
            dma((quarters,)),
            dma((quarters,)),
            dma((quarters,)),
            dma((quarters,)),
            dma((BACK * quarters,)),
            dma((BACK * quarters,)),
            dma((quarters,)),
            dma((quarters,)),
            dma((len(given),)),
        ] + [pltpu.VMEM(one.shape, one.dtype) for one in given] + [
        ],
        compiler_params=pltpu.CompilerParams(
            collective_id=0, has_side_effects=True, vmem_limit_bytes=46 * 1024 * 1024
        ),
    )(*(pltpu.with_memory_space_constraint(one, pltpu.HBM) for one in (forcing, coarse_guess, initial) + given))
    return out, gap.reshape(1, N, 16, N)


def solution(mesh):
    in_specs = (P("tm", "space", None, None), P("tm", "space", None, None), P("space", None, None))
    out_specs = (P("tm", "space", None, None), P("tm", None, "space", None))
    return jax.shard_map(per_device, mesh=mesh, in_specs=in_specs, out_specs=out_specs, check_vma=False)
```

time: 158 us -> 134 us (0.85)
  Pallas kernels: 151 us -> 130 us
  local copies, waits for them, and re-layouts: 5.76 us -> 2.99 us
    pallas_call x1, Pallas kernels: 151 us -> 130 us  [per_device(): pl.pallas_call(kernel, out_shape=(jax.ShapeDtypeStruct((STEPS, 16, N, N),...]
    unnamed x4 -> x2, local copies, waits for them, and re-layouts: 5.76 us -> 2.99 us
where the time goes in v2:
time: 134 us
  Pallas kernels  130 us (97%)
  local copies, waits for them, and re-layouts  2.99 us (2%)
    pallas_call x1, Pallas kernels, per_device(): pl.pallas_call(kernel, out_shape=(jax.ShapeDtypeStruct((STEPS, 16, N, N),...  130 us
    unnamed x2, local copies, waits for them, and re-layouts  2.99 us

profile of v2, /device:TPU:1, one launch (start us, length us, event | category | flops | bytes accessed | tf_op | source)
XLA Modules:
  0.0 134.1 jit_solution(4070726588418138152)
XLA Ops:
  0.6 130.5 %shard_map.113 = (f32[4,16,128,128]{3,2,1,0:T(8,128)S(1)}, f32[2048,128]{1,0:T(8,128)S(1)}) custom-call(f32[4,16,128,128]{3,2,1,0:T(8,128)} %forcing_ref.1, f32[1,16,128,128]{3,2,1,0:T(8,128)} %guess_ref.1, f32[16,128,128]{2,1,0:T(8,128)} %initial_ref.1, bf16[256,256]{1,0:T(8,128)(2,1)} %constant.14.clone.refs_0_, bf16[256,256]{1,0:T(8,128)(2,1)} %constant.15.clone.refs_1_, ...), custom_call_target="tpu_custom_call" | custom-call | tf_op jit(solution)/shard_map/pallas_call | solution.py:474
  131.1 2.0 %copy.14 = f32[4,16,128,128]{3,2,1,0:T(8,128)} copy(f32[4,16,128,128]{3,2,1,0:T(8,128)S(1)} %get-tuple-element.8) | data formatting | bytes 8388608
  133.2 1.0 copy.15

commit v3 on v2

--- a/solution.py
+++ b/solution.py
@@ -15,9 +15,9 @@
 TIME_STEP = 0.5
 HALVES = 2
 PAIRS = 4
-CHUNKS = 2
-GROUP = PAIRS // CHUNKS
-ROWS = N * GROUP // TM
+PIECES = HALVES * PAIRS
+SHARE = TM // 2
+ROWS = N // SHARE
 FIELDS = 4
 BACK = 3
 HALF_STEP = 0.5 * TIME_STEP
@@ -49,7 +49,7 @@
     sine = sine_table(N)
     left = left_table(sine)
     right = np.ascontiguousarray(left.T)
-    chosen = sine.reshape(SPACE, HALVES, CHUNKS, GROUP, 2, N).transpose(3, 0, 1, 2, 4, 5).reshape(GROUP, 64, N)
+    chosen = sine.reshape(SPACE, HALVES, PAIRS, 2, N).transpose(3, 0, 1, 2, 4).reshape(2, 64, N)
     anchor_y = left_table(chosen)
     anchor_x = left_table(sine.reshape(N // ROWS, ROWS, N))
     beside = np.zeros((2, SPACE, N))
@@ -90,7 +90,7 @@
     load_sem, x_send, x_recv, plane_send, plane_recv, anchor_send, anchor_recv, shift_send, shift_recv,
     change_send, change_recv, scan_send, scan_recv, error_send, error_recv, back_send, back_recv,
     beside_send, beside_recv,
-    table_sem, right_ref, left_ref, anchor_y_ref, anchor_x_ref, beside_ref, plane_ref, along_y_ref,
+    entered, table_sem, right_ref, left_ref, anchor_y_ref, anchor_x_ref, beside_ref, plane_ref, along_y_ref,
     ) = refs[:7], refs[7:]
     tables_here = (right_ref, left_ref, anchor_y_ref, anchor_x_ref, beside_ref, plane_ref, along_y_ref)
     t, s = lax.axis_index("tm"), lax.axis_index("space")
@@ -99,13 +99,18 @@
 
     barrier = pltpu.get_barrier_semaphore()
 
-    @pl.loop(0, TM - 1)
-    def _(k):
-        far = 1 + lax.rem(k + 15, TM - 1)
-        pl.semaphore_signal(barrier, inc=1, device_id=(lax.rem(t + far, TM), s), device_id_type=MESH)
-
     for k in range(1, SPACE):
         pl.semaphore_signal(barrier, inc=1, device_id=(t, lax.rem(s + k, SPACE)), device_id_type=MESH)
+    for other in (after, lax.rem(t + TM - 1, TM)):
+        pl.semaphore_signal(barrier, inc=1, device_id=(other, s), device_id_type=MESH)
+
+    def tell(r):
+        for by in (1 << r, TM - (1 << r)):
+            pl.semaphore_signal(entered.at[r], inc=1, device_id=(lax.rem(t + by, TM), s), device_id_type=MESH)
+
+    def hear(r):
+        pl.semaphore_wait(entered.at[r], 2)
+
 
     loads = [pltpu.make_async_copy(guess_ref.at[0], cells.at[0], load_sem.at[0])]
     loads += [pltpu.make_async_copy(forcing_ref.at[k], cells.at[k + 1], load_sem.at[k + 1]) for k in range(STEPS)]
@@ -188,7 +193,7 @@
     loads[2].wait()
     loads[3].wait()
     gap_cells[pl.ds(1, 16)] = cells[2] - cells[3]
-    pl.semaphore_wait(barrier, SPACE - 1 + TM - 1)
+    pl.semaphore_wait(barrier, SPACE - 1 + 2)
     exchange(0, 0)
     exchange(0, 1)
     planes = [
@@ -197,12 +202,17 @@
     ]
     for plane in planes:
         plane.start()
+    tell(0)
     loads[1].wait()
     to_modes(1, 1)
     exchange(1, 0)
+    hear(0)
+    tell(1)
     loads[4].wait()
     to_modes(4, 2)
     exchange(2, 0)
+    hear(1)
+    tell(2)
     pass_guess(0)
     for plane in planes:
         plane.wait_recv()
@@ -210,11 +220,15 @@
     gap_cells[17] = jnp.where(s == SPACE - 1, jnp.zeros((N, N), F32), gap_cells[17])
     middle_to_modes(3)
     exchange(3, 0)
+    hear(2)
+    tell(3)
     pass_guess(1)
+    hear(3)
 
     loads[5].wait()
-    column, block_of = lax.div(t, TM // GROUP), lax.rem(t, TM // GROUP)
+    column, block_of = lax.div(t, SHARE), lax.rem(t, SHARE)
     mine = pl.ds(pl.multiple_of(ROWS * block_of, ROWS), ROWS)
+    line = pl.ds(pl.multiple_of(N * column, N), N)
 
     @pl.loop(0, 4, unroll=True)
     def _(i):
@@ -247,10 +261,10 @@
         wide = STEPS * HALF_STEP
         coarse[h, pair] = (1.0 + wide * spectrum) / (1.0 - wide * spectrum)
 
-    def pass_change(h, c):
-        at, pairs = CHUNKS * h + c, pl.ds(GROUP * c, GROUP)
+    def pass_change(h, pair):
+        at = PAIRS * h + pair
         remote(
-            change.at[h, pairs], change_before.at[h, pairs], change_send.at[at], change_recv.at[at], after, s
+            change.at[h, pair], change_before.at[h, pair], change_send.at[at], change_recv.at[at], after, s
         ).start()
 
     def relax(h):
@@ -268,42 +282,39 @@
 
         whole_lines(6 + h)
         arrived(begin.at[h], shift_send.at[h], shift_recv.at[h])
-        for c in range(CHUNKS):
-
-            @pl.loop(GROUP * c, GROUP * (c + 1), unroll=True)
-            def _(pair):
-                rate, scale = fine[h, pair], weight[h, pair]
-                square = rate * rate
-                third = along_columns(left_ref[...], lines(6 + h, pair)) * (scale * scale * (1.0 / TIME_STEP))
-                third = third + square * parts[0, h, pair]
-                parts[1, h, pair] = third
-                value = parts[2, h, pair] + rate * third
-                value = square * square * begin[h, pair] + value
-                parts[2, h, pair] = value
-                known = guess[h, pair]
-                change[h, pair] = jnp.where(t == TM - 1, known, value - known)
-
-            at = CHUNKS * h + c
+        for pair in range(PAIRS):
+            rate, scale = fine[h, pair], weight[h, pair]
+            square = rate * rate
+            third = along_columns(left_ref[...], lines(6 + h, pair)) * (scale * scale * (1.0 / TIME_STEP))
+            third = third + square * parts[0, h, pair]
+            parts[1, h, pair] = third
+            value = parts[2, h, pair] + rate * third
+            value = square * square * begin[h, pair] + value
+            parts[2, h, pair] = value
+            known = guess[h, pair]
+            change[h, pair] = jnp.where(t == TM - 1, known, value - known)
+            at = PAIRS * h + pair
 
             @pl.loop(0, TM - 1)
             def _(k):
                 far = 1 + lax.rem(k + 15, TM - 1)
                 other = lax.rem(t + far, TM)
-                rows = pl.ds(pl.multiple_of(ROWS * lax.rem(other, TM // GROUP), ROWS), ROWS)
+                rows = pl.ds(pl.multiple_of(ROWS * lax.rem(other, SHARE), ROWS), ROWS)
+                lanes = pl.ds(pl.multiple_of(N * lax.div(other, SHARE), N), N)
                 remote(
-                    change.at[h, GROUP * c + lax.div(other, TM // GROUP), rows], scan_in.at[at, t],
+                    change.at[h, pair, rows, lanes], scan_in.at[at, t],
                     scan_send.at[at], scan_recv.at[at], other, s,
                 ).start()
 
-            scan_in[at, t] = change[h, GROUP * c + column, mine, :]
+            scan_in[at, t] = change[h, pair, mine, line]
         pass_change(h, 0)
 
-    def scan(h, c):
-        at = CHUNKS * h + c
+    def scan(h, pair):
+        at = PAIRS * h + pair
         arrived(scan_in.at[at, pl.ds(0, TM - 1)], scan_send.at[at], scan_recv.at[at])
-        one = fine[h, GROUP * c + column, mine, :]
+        one = fine[h, pair, mine, line]
         square = one * one
-        power, rate = square * square, coarse[h, GROUP * c + column, mine, :]
+        power, rate = square * square, coarse[h, pair, mine, line]
         first = anchor[at] - scan_in[at, TM - 1]
         scan_out[at, 0] = first
 
@@ -318,83 +329,98 @@
             far = 1 + lax.rem(k + 15, TM - 1)
             other = lax.rem(t + far, TM)
             remote(
-                scan_out.at[at, other], error_before.at[h, GROUP * c + column, mine],
+                scan_out.at[at, other], error_before.at[h, pair, mine, line],
                 error_send.at[at], error_recv.at[at], other, s,
             ).start()
 
-        error_before[h, GROUP * c + column, mine, :] = scan_out[at, t]
-
-    def go_back(h, c):
-        at, pairs = CHUNKS * h + c, pl.ds(GROUP * c, GROUP)
-        arrived(change_before.at[h, pairs], change_send.at[at], change_recv.at[at])
+        error_before[h, pair, mine, line] = scan_out[at, t]
+
+    def go_back(h, pair):
+        at = PAIRS * h + pair
+        quarter, i = at // 2, pair % 2
+        arrived(change_before.at[h, pair], change_send.at[at], change_recv.at[at])
         arrived(scan_out.at[at, pl.ds(0, TM - 1)], error_send.at[at], error_recv.at[at])
-
-        @pl.loop(0, GROUP, unroll=True)
-        def _(i):
-            pair = GROUP * c + i
-            came = error_before[h, pair]
-            delta = jnp.where(t == 0, came, change_before[h, pair])
-            error = jnp.where(t == 0, jnp.zeros_like(came), came)
-            rate = fine[h, pair]
-            square = rate * rate
-            gap = square * square * delta
+        came = error_before[h, pair]
+        delta = jnp.where(t == 0, came, change_before[h, pair])
+        error = jnp.where(t == 0, jnp.zeros_like(came), came)
+        rate = fine[h, pair]
+        square = rate * rate
+        gap = square * square * delta
+        for u in range(2):
+            residual_ref[pl.ds(8 * h + 2 * pair + u, N, stride=16), :] = gap[:, u * N : (u + 1) * N]
+        start = begin[h, pair] + (delta + error)
+        first = rate * start + parts[0, h, pair]
+        third = rate * square * start + parts[1, h, pair]
+        last = parts[2, h, pair] + (gap + coarse[h, pair] * error)
+        for k, point in enumerate((first, third, last)):
+            point = along_columns(left_ref[...], point)
             for u in range(2):
-                residual_ref[pl.ds(8 * h + 2 * pair + u, N, stride=16), :] = gap[:, u * N : (u + 1) * N]
-            start = begin[h, pair] + (delta + error)
-            first = rate * start + parts[0, h, pair]
-            third = rate * square * start + parts[1, h, pair]
-            last = parts[2, h, pair] + (gap + coarse[h, pair] * error)
-            for k, point in enumerate((first, third, last)):
-                point = along_columns(left_ref[...], point)
-                for u in range(2):
-                    rows = pl.ds(pl.multiple_of(32 * i + 16 * u, 16), 16)
-                    back_sent[4 * k + at, :, rows, :] = point[:, u * N : (u + 1) * N].reshape(SPACE, 16, N)
-            point = along_columns(beside_ref[...], first - third)
-            for u in range(2):
-                for side in range(2):
-                    rows = pl.ds(4 * i + 2 * u + side, 8, stride=8)
-                    beside_sent[at, rows, :] = point[8 * side : 8 * side + 8, u * N : (u + 1) * N]
+                back_sent[PIECES * k + at, :, pl.ds(16 * u, 16), :] = point[:, u * N : (u + 1) * N].reshape(SPACE, 16, N)
+        point = along_columns(beside_ref[...], first - third)
+        for u in range(2):
+            for side in range(2):
+                rows = pl.ds(4 * i + 2 * u + side, 8, stride=8)
+                beside_sent[quarter, rows, :] = point[8 * side : 8 * side + 8, u * N : (u + 1) * N]
 
         for k in range(BACK):
-            slot = pl.ds(pl.multiple_of(256 * s + 64 * at, 64), 64)
+            slot = pl.ds(pl.multiple_of(256 * s + 32 * at, 32), 32)
             for hop in range(1, SPACE):
                 other = lax.rem(s + hop, SPACE)
                 remote(
-                    back_sent.at[4 * k + at, other], back_received.at[k, slot],
-                    back_send.at[4 * k + at], back_recv.at[4 * k + at], t, other,
+                    back_sent.at[PIECES * k + at, other], back_received.at[k, slot],
+                    back_send.at[PIECES * k + at], back_recv.at[PIECES * k + at], t, other,
                 ).start()
-            back_received[k, slot, :] = back_sent[4 * k + at, s]
-            if k == 1:
-                slot = pl.ds(pl.multiple_of(32 * s + 8 * at, 8), 8)
+            back_received[k, slot, :] = back_sent[PIECES * k + at, s]
+            if k == 1 and i == 1:
+                slot = pl.ds(pl.multiple_of(32 * s + 8 * quarter, 8), 8)
                 for hop in range(1, SPACE):
                     other = lax.rem(s + hop, SPACE)
                     remote(
-                        beside_sent.at[at, pl.ds(pl.multiple_of(8 * other, 8), 8)], beside_received.at[slot],
-                        beside_send.at[at], beside_recv.at[at], t, other,
+                        beside_sent.at[quarter, pl.ds(pl.multiple_of(8 * other, 8), 8)], beside_received.at[slot],
+                        beside_send.at[quarter], beside_recv.at[quarter], t, other,
                     ).start()
-                beside_received[slot, :] = beside_sent[at, pl.ds(pl.multiple_of(8 * s, 8), 8), :]
+                beside_received[slot, :] = beside_sent[quarter, pl.ds(pl.multiple_of(8 * s, 8), 8), :]
 
     relax(0)
     arrived(anchor_received.at[pl.ds(0, SPACE - 1)], anchor_send, anchor_recv)
-    for at in range(HALVES * CHUNKS):
-        both = jnp.concatenate(
-            [anchor_received[:, pl.ds(32 * at + 16 * u, 16), :].reshape(N, N) for u in range(2)], axis=1
-        )
+    for at in range(PIECES):
+        both = anchor_received[:, pl.ds(16 * at, 16), :].reshape(N, N)
         anchor[at] = along_columns(anchor_x_ref[block_of], both)
-    scan(0, 0)
-    pass_change(0, 1)
-    scan(0, 1)
+    for pair in range(PAIRS):
+        scan(0, pair)
+        if pair + 2 < PAIRS:
+            pass_change(0, pair + 1)
+    pass_change(0, PAIRS - 1)
     relax(1)
-    go_back(0, 0)
-    go_back(0, 1)
-    scan(1, 0)
-    pass_change(1, 1)
-    scan(1, 1)
-    go_back(1, 0)
-    go_back(1, 1)
+    for pair in range(PAIRS):
+        go_back(0, pair)
+    for pair in range(PAIRS):
+        scan(1, pair)
+        if pair + 2 < PAIRS:
+            pass_change(1, pair + 1)
+    pass_change(1, PAIRS - 1)
+    for pair in range(PAIRS):
+        go_back(1, pair)
+
+    for at in range(2 * FIELDS):
+        left_here(received.at[at, pl.ds(0, 7 * N)], x_send.at[at], x_recv.at[at])
+    for plane in planes:
+        plane.wait_send()
+    left_here(anchor_received.at[pl.ds(0, SPACE - 1)], anchor_send, anchor_recv)
+    for h in range(HALVES):
+        left_here(guess.at[h], shift_send.at[h], shift_recv.at[h])
+    for at in range(PIECES):
+        left_here(change.at[0, 0], change_send.at[at], change_recv.at[at])
+        left_here(scan_in.at[at, pl.ds(0, TM - 1)], scan_send.at[at], scan_recv.at[at])
+        left_here(scan_out.at[at, pl.ds(0, TM - 1)], error_send.at[at], error_recv.at[at])
+    for k in range(BACK):
+        for at in range(PIECES * k, PIECES * (k + 1) - 1):
+            left_here(back_received.at[0, pl.ds(0, 7 * 32)], back_send.at[at], back_recv.at[at])
+
     def back(k):
-        for at in range(HALVES * CHUNKS):
-            arrived(back_received.at[k, pl.ds(0, 7 * 64)], back_send.at[4 * k + at], back_recv.at[4 * k + at])
+        for at in range(PIECES):
+            here = PIECES * k + at
+            arrived(back_received.at[k, pl.ds(0, 7 * 32)], back_send.at[here], back_recv.at[here])
 
     def columns_at(k, x):
         return jnp.concatenate([back_received[k, pl.ds(x + u, N, stride=16), :] for u in range(2)], axis=1)
@@ -415,7 +441,7 @@
             solution_ref[step, pl.ds(4 * i, 4)] = block.reshape(4, N, N)
 
 
-    for at in range(HALVES * CHUNKS):
+    for at in range(PIECES // 2):
         arrived(beside_received.at[pl.ds(0, 7 * 8)], beside_send.at[at], beside_recv.at[at])
     both = jnp.concatenate([beside_received[pl.ds(side, N, stride=2), :] for side in range(2)], axis=1)
     beside_cells[pl.ds(0, 2)] = to_cells([both]).reshape(2, N, N)
@@ -448,25 +474,15 @@
         solution_ref[3, pl.ds(4 * i, 4)] = block.reshape(4, N, N)
 
 
-    for at in range(2 * FIELDS):
-        left_here(received.at[at, pl.ds(0, 7 * N)], x_send.at[at], x_recv.at[at])
-    for plane in planes:
-        plane.wait_send()
-    left_here(anchor_received.at[pl.ds(0, SPACE - 1)], anchor_send, anchor_recv)
-    for h in range(HALVES):
-        left_here(guess.at[h], shift_send.at[h], shift_recv.at[h])
-    for at in range(HALVES * CHUNKS):
-        left_here(change.at[0, pl.ds(0, GROUP)], change_send.at[at], change_recv.at[at])
-        left_here(scan_in.at[at, pl.ds(0, TM - 1)], scan_send.at[at], scan_recv.at[at])
-        left_here(scan_out.at[at, pl.ds(0, TM - 1)], error_send.at[at], error_recv.at[at])
+    for at in range(PIECES // 2):
         left_here(beside_received.at[pl.ds(0, 7 * 8)], beside_send.at[at], beside_recv.at[at])
-    for at in range(BACK * HALVES * CHUNKS):
-        left_here(back_received.at[0, pl.ds(0, 7 * 64)], back_send.at[at], back_recv.at[at])
-
+    for k in range(BACK):
+        at = PIECES * (k + 1) - 1
+        left_here(back_received.at[0, pl.ds(0, 7 * 32)], back_send.at[at], back_recv.at[at])
 
 def per_device(forcing, coarse_guess, initial):
     modal = (HALVES, PAIRS, N, 2 * N)
-    quarters = HALVES * CHUNKS
+    quarters = PIECES // 2
     dma = pltpu.SemaphoreType.DMA
     vmem = pl.BlockSpec(memory_space=pltpu.VMEM)
     anywhere = pl.BlockSpec(memory_space=pltpu.HBM)
@@ -488,7 +504,7 @@
             pltpu.VMEM((1024, N), F32),
             pltpu.VMEM((SPACE, N, N), F32),
             pltpu.VMEM((SPACE, N, N), F32),
-            pltpu.VMEM((quarters, ROWS, 2 * N), F32),
+            pltpu.VMEM((PIECES, ROWS, N), F32),
             pltpu.VMEM(modal, F32),
             pltpu.VMEM(modal, F32),
             pltpu.VMEM(modal, F32),
@@ -497,10 +513,10 @@
             pltpu.VMEM((3,) + modal, F32),
             pltpu.VMEM(modal, F32),
             pltpu.VMEM(modal, F32),
-            pltpu.VMEM((quarters, TM, ROWS, 2 * N), F32),
-            pltpu.VMEM((quarters, TM, ROWS, 2 * N), F32),
-            pltpu.VMEM(modal, F32),
-            pltpu.VMEM((BACK * quarters, SPACE, 64, N), F32),
+            pltpu.VMEM((PIECES, TM, ROWS, N), F32),
+            pltpu.VMEM((PIECES, TM, ROWS, N), F32),
+            pltpu.VMEM(modal, F32),
+            pltpu.VMEM((BACK * PIECES, SPACE, 32, N), F32),
             pltpu.VMEM((BACK, 16 * N, N), F32),
             pltpu.VMEM((quarters, 64, N), F32),
             pltpu.VMEM((2 * N, N), F32),
@@ -514,16 +530,17 @@
             dma,
             dma((HALVES,)),
             dma((HALVES,)),
+            dma((PIECES,)),
+            dma((PIECES,)),
+            dma((PIECES,)),
+            dma((PIECES,)),
+            dma((PIECES,)),
+            dma((PIECES,)),
+            dma((BACK * PIECES,)),
+            dma((BACK * PIECES,)),
             dma((quarters,)),
             dma((quarters,)),
-            dma((quarters,)),
-            dma((quarters,)),
-            dma((quarters,)),
-            dma((quarters,)),
-            dma((BACK * quarters,)),
-            dma((BACK * quarters,)),
-            dma((quarters,)),
-            dma((quarters,)),
+            pltpu.SemaphoreType.REGULAR((4,)),
             dma((len(given),)),
         ] + [pltpu.VMEM(one.shape, one.dtype) for one in given] + [
         ],

time: 134 us -> 130 us (0.970)
  Pallas kernels: 130 us -> 126 us
    pallas_call x1, Pallas kernels: 130 us -> 126 us  [per_device(): pl.pallas_call(kernel, out_shape=(jax.ShapeDtypeStruct((STEPS, 16, N, N),...]
where the time goes in v3:
time: 130 us
  Pallas kernels  126 us (97%)
  local copies, waits for them, and re-layouts  2.99 us (2%)
    pallas_call x1, Pallas kernels, per_device(): pl.pallas_call(kernel, out_shape=(jax.ShapeDtypeStruct((STEPS, 16, N, N),...  126 us
    unnamed x2, local copies, waits for them, and re-layouts  2.99 us

profile of v3, /device:TPU:1, one launch (start us, length us, event | category | flops | bytes accessed | tf_op | source)
XLA Modules:
  0.0 129.5 jit_solution(3329070299437865804)
XLA Ops:
  0.6 125.9 %shard_map.113 = (f32[4,16,128,128]{3,2,1,0:T(8,128)S(1)}, f32[2048,128]{1,0:T(8,128)S(1)}) custom-call(f32[4,16,128,128]{3,2,1,0:T(8,128)} %forcing_ref.1, f32[1,16,128,128]{3,2,1,0:T(8,128)} %guess_ref.1, f32[16,128,128]{2,1,0:T(8,128)} %initial_ref.1, bf16[256,256]{1,0:T(8,128)(2,1)} %constant.14.clone.refs_0_, bf16[256,256]{1,0:T(8,128)(2,1)} %constant.15.clone.refs_1_, ...), custom_call_target="tpu_custom_call" | custom-call | tf_op jit(solution)/shard_map/pallas_call | solution.py:490
  126.5 2.0 %copy.14 = f32[4,16,128,128]{3,2,1,0:T(8,128)} copy(f32[4,16,128,128]{3,2,1,0:T(8,128)S(1)} %get-tuple-element.8) | data formatting | bytes 8388608
  128.6 1.0 copy.15

commit v4 on v3

--- a/solution.py
+++ b/solution.py
@@ -399,8 +399,35 @@
         if pair + 2 < PAIRS:
             pass_change(1, pair + 1)
     pass_change(1, PAIRS - 1)
-    for pair in range(PAIRS):
+    def back(k, pieces):
+        for at in pieces:
+            here = PIECES * k + at
+            arrived(back_received.at[k, pl.ds(0, 7 * 32)], back_send.at[here], back_recv.at[here])
+
+    def middle_rows(first, count):
+        for other in range(SPACE):
+            rows = pl.ds(256 * other + 32 * first, 32 * count)
+            gap = (back_received[0, rows, :] - back_received[1, rows, :]).reshape(2 * count, 16, N)
+            scale = plane_ref[pl.ds(16 * other + 2 * first, 2 * count), pl.ds(0, N)]
+            back_received[BACK, rows, :] = (gap * scale[:, None, :]).reshape(32 * count, N)
+
+    def rows_to_cells(k, first, count):
+        parts_of = [pl.ds(256 * other + 32 * first, 32 * count) for other in range(SPACE)]
+        for four in (parts_of[:4], parts_of[4:]):
+            block = jnp.concatenate([back_received[k, rows, :] for rows in four], axis=0)
+            block = along_rows(block, right_ref)
+            for n, rows in enumerate(four):
+                back_received[k, rows, :] = block[32 * count * n : 32 * count * (n + 1)]
+
+    for pair in range(PAIRS - 1):
         go_back(1, pair)
+    early, late = range(5), range(5, PIECES)
+    for k in range(BACK):
+        back(k, early)
+    middle_rows(0, 5)
+    for k in range(BACK + 1):
+        rows_to_cells(k, 0, 5)
+    go_back(1, PAIRS - 1)
 
     for at in range(2 * FIELDS):
         left_here(received.at[at, pl.ds(0, 7 * N)], x_send.at[at], x_recv.at[at])
@@ -417,34 +444,32 @@
         for at in range(PIECES * k, PIECES * (k + 1) - 1):
             left_here(back_received.at[0, pl.ds(0, 7 * 32)], back_send.at[at], back_recv.at[at])
 
-    def back(k):
-        for at in range(PIECES):
-            here = PIECES * k + at
-            arrived(back_received.at[k, pl.ds(0, 7 * 32)], back_send.at[here], back_recv.at[here])
-
     def columns_at(k, x):
         return jnp.concatenate([back_received[k, pl.ds(x + u, N, stride=16), :] for u in range(2)], axis=1)
 
-    def to_cells(four):
-        pieces = []
-        for both in four:
-            both = along_columns(left_ref[...], both)
-            pieces += [both[:, :N], both[:, N:]]
-        return along_rows(jnp.concatenate(pieces, axis=0), right_ref)
-
+    def to_cells(k, x):
+        both = along_columns(left_ref[...], columns_at(k, x))
+        return both[:, :N], both[:, N:]
+
+    back(0, late)
+    back(1, late)
+    middle_rows(5, 3)
     for k, step in ((0, 0), (1, 2)):
-        back(k)
-
-        @pl.loop(0, 4, unroll=True)
+        rows_to_cells(k, 5, 3)
+
+        @pl.loop(0, 8, unroll=True)
         def _(i):
-            block = to_cells([columns_at(k, 4 * i + 2 * pair) for pair in range(2)])
-            solution_ref[step, pl.ds(4 * i, 4)] = block.reshape(4, N, N)
-
+            for u, one in enumerate(to_cells(k, 2 * i)):
+                solution_ref[step, 2 * i + u] = one
+
+    rows_to_cells(BACK, 5, 3)
 
     for at in range(PIECES // 2):
         arrived(beside_received.at[pl.ds(0, 7 * 8)], beside_send.at[at], beside_recv.at[at])
     both = jnp.concatenate([beside_received[pl.ds(side, N, stride=2), :] for side in range(2)], axis=1)
-    beside_cells[pl.ds(0, 2)] = to_cells([both]).reshape(2, N, N)
+    both = along_columns(left_ref[...], both)
+    both = along_rows(jnp.concatenate([both[:, :N], both[:, N:]], axis=0), right_ref)
+    beside_cells[pl.ds(0, 2)] = both.reshape(2, N, N)
 
     @pl.loop(0, 16)
     def _(x):
@@ -453,26 +478,21 @@
     beside_cells[18] = beside_cells[1]
     beside_cells[1] = beside_cells[0]
 
-    @pl.loop(0, 4, unroll=True)
+    @pl.loop(0, 8, unroll=True)
     def _(i):
-        four = [
-            (columns_at(0, 4 * i + 2 * pair) - columns_at(1, 4 * i + 2 * pair)) * plane_ref[...]
-            for pair in range(2)
-        ]
-        block = to_cells(four).reshape(4, N, N)
-        planes = pl.ds(4 * i, 4)
-        bent = beside_cells[pl.ds(4 * i + 1, 4)] + beside_cells[pl.ds(4 * i + 3, 4)]
-        bent = bent - 2.0 * beside_cells[pl.ds(4 * i + 2, 4)] + block
-        total = solution_ref[0, planes] + solution_ref[2, planes] + HALF_STEP * bent
-        solution_ref[1, planes] = 0.5 * total + HALF_STEP * gap_cells[pl.ds(4 * i + 1, 4)]
-
-    back(2)
-
-    @pl.loop(0, 4, unroll=True)
+        for u, one in enumerate(to_cells(BACK, 2 * i)):
+            x = 2 * i + u
+            bent = beside_cells[x + 1] + beside_cells[x + 3] - 2.0 * beside_cells[x + 2] + one
+            total = solution_ref[0, x] + solution_ref[2, x] + HALF_STEP * bent
+            solution_ref[1, x] = 0.5 * total + HALF_STEP * gap_cells[x + 1]
+
+    back(2, late)
+    rows_to_cells(2, 5, 3)
+
+    @pl.loop(0, 8, unroll=True)
     def _(i):
-        block = to_cells([columns_at(2, 4 * i + 2 * pair) for pair in range(2)])
-        solution_ref[3, pl.ds(4 * i, 4)] = block.reshape(4, N, N)
-
+        for u, one in enumerate(to_cells(2, 2 * i)):
+            solution_ref[3, 2 * i + u] = one
 
     for at in range(PIECES // 2):
         left_here(beside_received.at[pl.ds(0, 7 * 8)], beside_send.at[at], beside_recv.at[at])
@@ -517,7 +537,7 @@
             pltpu.VMEM((PIECES, TM, ROWS, N), F32),
             pltpu.VMEM(modal, F32),
             pltpu.VMEM((BACK * PIECES, SPACE, 32, N), F32),
-            pltpu.VMEM((BACK, 16 * N, N), F32),
+            pltpu.VMEM((BACK + 1, 16 * N, N), F32),
             pltpu.VMEM((quarters, 64, N), F32),
             pltpu.VMEM((2 * N, N), F32),
             pltpu.VMEM((19, N, N), F32),

time: 130 us -> 130 us (level)
  no operation moved by 1% of the time
where the time goes in v4:
time: 130 us
  Pallas kernels  126 us (97%)
  local copies, waits for them, and re-layouts  2.99 us (2%)
    pallas_call x1, Pallas kernels, per_device(): pl.pallas_call(kernel, out_shape=(jax.ShapeDtypeStruct((STEPS, 16, N, N),...  126 us
    unnamed x2, local copies, waits for them, and re-layouts  2.99 us

profile of v4, /device:TPU:1, one launch (start us, length us, event | category | flops | bytes accessed | tf_op | source)
XLA Modules:
  0.0 129.7 jit_solution(832471899888381872)
XLA Ops:
  0.6 126.1 %shard_map.113 = (f32[4,16,128,128]{3,2,1,0:T(8,128)S(1)}, f32[2048,128]{1,0:T(8,128)S(1)}) custom-call(f32[4,16,128,128]{3,2,1,0:T(8,128)} %forcing_ref.1, f32[1,16,128,128]{3,2,1,0:T(8,128)} %guess_ref.1, f32[16,128,128]{2,1,0:T(8,128)} %initial_ref.1, bf16[256,256]{1,0:T(8,128)(2,1)} %constant.14.clone.refs_0_, bf16[256,256]{1,0:T(8,128)(2,1)} %constant.15.clone.refs_1_, ...), custom_call_target="tpu_custom_call" | custom-call | tf_op jit(solution)/shard_map/pallas_call | solution.py:510
  126.7 2.0 %copy.14 = f32[4,16,128,128]{3,2,1,0:T(8,128)} copy(f32[4,16,128,128]{3,2,1,0:T(8,128)S(1)} %get-tuple-element.8) | data formatting | bytes 8388608
  128.7 1.0 copy.15
